TPU v7x, 512 devices: a 4x2x32 block of a 4x8x32 slice. The times are simulated.
512 devices in a mesh: parts: 2 (over y), shot: 32 (over z), freq: 4 (over x), rep: 2 (over core).
Axes of the slice: x: 4, y: 2, z: 32, core: 2. Of those that a mesh axis runs over, the one named last changes fastest.
The devices are a block of a 4x8x32 slice.
Arguments:
- recorded: bfloat16 [2, 8, 2048, 2048], P(None, ('parts', 'freq'), ('shot', 'rep')), parts along dimension 1, may hold values from -6 to 6
- receiver_x: float32 [4096], P('parts'), parts along dimension 0, may hold values from -12800 to 12800
- source_x: float32 [4096], P('parts'), parts along dimension 0, may hold values from -12800 to 12800
Outputs:
- predicted: bfloat16 [2, 8, 2048, 2048], P(None, ('parts', 'freq'), ('shot', 'rep')), parts along dimension 1
There are 2 independent parts, one for each index of `parts`. A program takes and returns all parts, laid end to end along the dimension named above; each array names one. Nothing has to cross between parts.
All inputs are finite; a program needn't handle non-finite values.
Results may differ from a plain program's by a relative error of at most 0.013.
Values may be sent and summed in bfloat16 or wider, within the bound.
No kernel may reach another device: no remote copies, remote signals or barrier semaphores. Data moves between devices by JAX's collectives and lax.ppermute only.
A program may use at most 64 MiB of HBM per device.

v0:
```python
import math

import jax
import jax.numpy as jnp
from jax import lax
from jax.sharding import PartitionSpec as P

NSLOW = 1024


two_pi = 6.283185307179586
base_hertz = 40.0
step_hertz = 0.5
slow_max = 0.0005


def from_partner(block, axis, distance):
    count = lax.axis_size(axis)
    route = []
    for low in range(count):
        high = low | 1 << distance
        if high != low and high < count:
            route += [(low, high), (high, low)]
    return lax.ppermute(block, axis, route)


def in_blocks(x, dim, peers):
    lengths = x.shape
    tiles = x.reshape(*lengths[:dim], peers, lengths[dim] // peers, *lengths[dim + 1 :])
    return jnp.moveaxis(tiles, dim, 0)


def laid_out(tiles, dim):
    tiles = jnp.moveaxis(tiles, 0, dim)
    lengths = tiles.shape
    return tiles.reshape(*lengths[:dim], lengths[dim] * lengths[dim + 1], *lengths[dim + 2 :])


def moved_by_axis(tiles, axes, sequence):
    lengths = [lax.axis_size(a) for a in axes]
    tiles = tiles.reshape(*lengths, *tiles.shape[1:])
    for k in sequence:
        tiles = lax.all_to_all(tiles, axes[k], split_axis=k, concat_axis=k, tiled=True)
    return tiles.reshape(-1, *tiles.shape[len(axes) :])


def exchange_by_chip(x, groups, sequence, split_dim, concat_dim):
    peers = lax.axis_size(groups[0]) * lax.axis_size(groups[1])
    tiles = in_blocks(x, split_dim, peers)
    return laid_out(moved_by_axis(tiles, groups, sequence), concat_dim)


def slowness_values(grid_count):
    counts = jnp.arange(grid_count, dtype=jnp.int32)
    return slow_max * ((2 * counts + 1 - grid_count).astype(jnp.float32) / grid_count)


def angle_columns(omegas, positions, slowness_grid):
    phases = (omegas[:, None] * slowness_grid[None, :])[:, None, :] * positions[None, :, None]
    return (jnp.cos(phases).astype(jnp.bfloat16), jnp.sin(phases).astype(jnp.bfloat16))


def angle_rows(omegas, positions, slowness_grid):
    phases = (omegas[:, None] * slowness_grid[None, :])[:, :, None] * positions[None, None, :]
    return (jnp.cos(phases).astype(jnp.bfloat16), jnp.sin(phases).astype(jnp.bfloat16))


def contract_product(form, left, right):
    return jnp.einsum(form, left, right, preferred_element_type=jnp.float32)


def receiver_forward(recorded, receiver_x, omegas, slowness_grid):
    data_real = recorded[0]
    data_imaginary = recorded[1]
    freq_count, shot_rows, rec_count = data_real.shape
    width_block = math.gcd(rec_count, 128)
    initial = jnp.zeros((freq_count, slowness_grid.shape[0], shot_rows), jnp.float32)

    def accumulate(loop_index, totals):
        first_row = loop_index * width_block
        positions = lax.dynamic_slice_in_dim(receiver_x, first_row, width_block, 0)
        cosine_lookup, sine_lookup = angle_columns(omegas, positions, slowness_grid)
        left_factor_real = lax.dynamic_slice_in_dim(data_real, first_row, width_block, 2)
        left_factor_imaginary = lax.dynamic_slice_in_dim(data_imaginary, first_row, width_block, 2)
        next_real = (
            totals[0]
            + contract_product("vqd,vdl->vlq", left_factor_real, cosine_lookup)
            + contract_product("vqd,vdl->vlq", left_factor_imaginary, sine_lookup)
        )
        next_imaginary = (
            totals[1]
            + contract_product("vqd,vdl->vlq", left_factor_imaginary, cosine_lookup)
            - contract_product("vqd,vdl->vlq", left_factor_real, sine_lookup)
        )
        return (next_real, next_imaginary)

    sum_real, sum_imaginary = lax.fori_loop(
        0, rec_count // width_block, accumulate, (initial, initial)
    )
    factor = 1.0 / math.sqrt(rec_count)
    return jnp.stack([sum_real * factor, sum_imaginary * factor], axis=1).astype(jnp.bfloat16)


def source_forward(gathered, source_x, omegas, slowness_grid):
    freq_count, parts_count, slice_rows, src_count = gathered.shape
    width_block = math.gcd(src_count, 128)
    initial = jnp.zeros((freq_count, slice_rows, slowness_grid.shape[0]), jnp.float32)

    def accumulate(loop_index, totals):
        first_row = loop_index * width_block
        positions = lax.dynamic_slice_in_dim(source_x, first_row, width_block, 0)
        cosine_lookup, sine_lookup = angle_columns(omegas, positions, slowness_grid)
        left_factor_real = lax.dynamic_slice_in_dim(gathered[:, 0], first_row, width_block, 2)
        left_factor_imaginary = lax.dynamic_slice_in_dim(gathered[:, 1], first_row, width_block, 2)
        next_real = (
            totals[0]
            + contract_product("fps,fsq->fpq", left_factor_real, cosine_lookup)
            + contract_product("fps,fsq->fpq", left_factor_imaginary, sine_lookup)
        )
        next_imaginary = (
            totals[1]
            + contract_product("fps,fsq->fpq", left_factor_imaginary, cosine_lookup)
            - contract_product("fps,fsq->fpq", left_factor_real, sine_lookup)
        )
        return (next_real, next_imaginary)

    sum_real, sum_imaginary = lax.fori_loop(
        0, src_count // width_block, accumulate, (initial, initial)
    )
    factor = 1.0 / math.sqrt(src_count)
    return ((sum_real * factor).astype(jnp.bfloat16), (sum_imaginary * factor).astype(jnp.bfloat16))


def tile_square(plane_real, plane_imaginary):
    freq_count, rows_local, slow_count = plane_real.shape
    shot_count = lax.axis_size("shot")
    copies = lax.axis_size("rep")
    bit_count = shot_count.bit_length() - 1
    levels = (bit_count + 1) // 2
    group = 1 << levels
    high_count = shot_count // group
    block_cols = slow_count // group
    shot_index = lax.axis_index("shot")
    low_index = jnp.bitwise_and(shot_index, group - 1)
    owned = jnp.stack([plane_real, plane_imaginary], axis=1)
    row_partition = owned
    for level in range(levels):
        partner_rows = from_partner(row_partition, "shot", level)
        upper = jnp.bitwise_and(jnp.right_shift(shot_index, level), 1) == 1
        row_partition = jnp.where(
            upper,
            jnp.concatenate([partner_rows, row_partition], axis=2),
            jnp.concatenate([row_partition, partner_rows], axis=2),
        )
    blocks = owned.reshape(freq_count, 2, rows_local, 1, group, 1, block_cols)
    outgoing = jnp.broadcast_to(
        blocks, (freq_count, 2, rows_local, high_count, group, copies, block_cols)
    )
    outgoing = outgoing.reshape(freq_count, 2, rows_local, high_count * group * copies * block_cols)
    columns = exchange_by_chip(outgoing, ("shot", "rep"), (1, 0), 3, 2)
    tile_real = contract_product(
        "fpk,fkq->fpq", row_partition[:, 0], columns[:, 0]
    ) - contract_product("fpk,fkq->fpq", row_partition[:, 1], columns[:, 1])
    tile_imaginary = contract_product(
        "fpk,fkq->fpq", row_partition[:, 0], columns[:, 1]
    ) + contract_product("fpk,fkq->fpq", row_partition[:, 1], columns[:, 0])
    factor = 1.0 / math.sqrt(NSLOW)
    tile = jnp.stack([tile_real * factor, tile_imaginary * factor], axis=1).astype(jnp.bfloat16)
    relative_offset = jnp.bitwise_xor(low_index, jnp.arange(group, dtype=jnp.int32))
    buffer = jnp.take(
        tile.reshape(freq_count, 2, group, rows_local, block_cols), relative_offset, axis=2
    )
    for level in range(levels):
        stride = 1 << level
        shaped = buffer.reshape(
            freq_count, 2, group // (2 * stride), 2, stride, rows_local, block_cols
        )
        arrived = from_partner(shaped[:, :, :, 1], "shot", level)
        buffer = jnp.concatenate([shaped[:, :, :, 0:1], arrived[:, :, :, None]], axis=3)
        buffer = buffer.reshape(freq_count, 2, group, rows_local, block_cols)
    ordered = jnp.take(buffer, relative_offset, axis=2)
    ordered = jnp.transpose(ordered, (0, 1, 3, 2, 4)).reshape(freq_count, 2, rows_local, slow_count)
    return (ordered[:, 0], ordered[:, 1])


def source_inverse(multiple_real, multiple_imaginary, source_x, omegas, slowness_grid):
    freq_count, slice_rows, slow_count = multiple_real.shape
    src_count = source_x.shape[0]
    width_block = math.gcd(slow_count, 128)
    initial = jnp.zeros((freq_count, slice_rows, src_count), jnp.float32)

    def accumulate(loop_index, totals):
        first_row = loop_index * width_block
        block_slowness = lax.dynamic_slice_in_dim(slowness_grid, first_row, width_block, 0)
        cosine_lookup, sine_lookup = angle_rows(omegas, source_x, block_slowness)
        left_factor_real = lax.dynamic_slice_in_dim(multiple_real, first_row, width_block, 2)
        left_factor_imaginary = lax.dynamic_slice_in_dim(
            multiple_imaginary, first_row, width_block, 2
        )
        next_real = (
            totals[0]
            + contract_product("fpq,fqs->fps", left_factor_real, cosine_lookup)
            - contract_product("fpq,fqs->fps", left_factor_imaginary, sine_lookup)
        )
        next_imaginary = (
            totals[1]
            + contract_product("fpq,fqs->fps", left_factor_real, sine_lookup)
            + contract_product("fpq,fqs->fps", left_factor_imaginary, cosine_lookup)
        )
        return (next_real, next_imaginary)

    sum_real, sum_imaginary = lax.fori_loop(
        0, slow_count // width_block, accumulate, (initial, initial)
    )
    factor = 1.0 / math.sqrt(NSLOW)
    return jnp.stack([sum_real * factor, sum_imaginary * factor], axis=1).astype(jnp.bfloat16)


def receiver_inverse(returned, receiver_x, omegas, slowness_grid):
    freq_count, parts_count, slow_count, shot_rows = returned.shape
    rec_count = receiver_x.shape[0]
    width_block = math.gcd(slow_count, 128)
    initial = jnp.zeros((freq_count, shot_rows, rec_count), jnp.float32)

    def accumulate(loop_index, totals):
        first_row = loop_index * width_block
        block_slowness = lax.dynamic_slice_in_dim(slowness_grid, first_row, width_block, 0)
        cosine_lookup, sine_lookup = angle_rows(omegas, receiver_x, block_slowness)
        left_factor_real = lax.dynamic_slice_in_dim(returned[:, 0], first_row, width_block, 1)
        left_factor_imaginary = lax.dynamic_slice_in_dim(returned[:, 1], first_row, width_block, 1)
        next_real = (
            totals[0]
            + contract_product("kom,kox->kmx", left_factor_real, cosine_lookup)
            - contract_product("kom,kox->kmx", left_factor_imaginary, sine_lookup)
        )
        next_imaginary = (
            totals[1]
            + contract_product("kom,kox->kmx", left_factor_real, sine_lookup)
            + contract_product("kom,kox->kmx", left_factor_imaginary, cosine_lookup)
        )
        return (next_real, next_imaginary)

    sum_real, sum_imaginary = lax.fori_loop(
        0, slow_count // width_block, accumulate, (initial, initial)
    )
    factor = 1.0 / math.sqrt(NSLOW)
    return jnp.stack([sum_real * factor, sum_imaginary * factor], axis=0).astype(jnp.bfloat16)


def body(recorded, receiver_x, source_x):
    per_device = recorded.shape[1]
    first_freq = lax.axis_index("freq") * per_device
    indices = (first_freq + jnp.arange(per_device, dtype=jnp.int32)).astype(jnp.float32)
    omegas = two_pi * (base_hertz + step_hertz * indices)
    slowness_grid = slowness_values(NSLOW)
    spread = receiver_forward(recorded, receiver_x, omegas, slowness_grid)
    gathered = exchange_by_chip(spread, ("shot", "rep"), (0, 1), 2, 3)
    plane_real, plane_imaginary = source_forward(gathered, source_x, omegas, slowness_grid)
    multiple_real, multiple_imaginary = tile_square(plane_real, plane_imaginary)
    back = source_inverse(multiple_real, multiple_imaginary, source_x, omegas, slowness_grid)
    returned = exchange_by_chip(back, ("shot", "rep"), (0, 1), 3, 2)
    return receiver_inverse(returned, receiver_x, omegas, slowness_grid)


def solution(mesh):
    return jax.shard_map(
        body,
        mesh=mesh,
        in_specs=(P(None, ("parts", "freq"), ("shot", "rep"), None), P("parts"), P("parts")),
        out_specs=P(None, ("parts", "freq"), ("shot", "rep"), None),
        check_vma=False,
    )
```

profile of v0, /device:TPU:33, one launch (start us, length us, event | category | flops | bytes accessed | tf_op | source)
XLA Modules:
  0.0 756.3 jit_solution(18356928895202269384)
XLA Ops:
  1.7 122.5 %while.64 = (s32[]{:T(128)}, f32[1,1024,32]{1,2,0:T(8,128)S(1)}, f32[1,1024,32]{1,2,0:T(8,128)S(1)}, f32[1]{0:T(128)}, f32[2048]{0:T(1024)S(1)}, /*index=5*/bf16...) while((s32[]{:T(128)}, f32[1,1024,32]{1,2,0:T(8,128)S(1)}, ...), condition=%wide.region_1.0_spmd.clone, body=%wide.region_0.0_spmd.clone.sunk | while | flops 34803720 | bytes 1105106 | solution.py:97
  126.0 46.3 %all-to-all-start = ((bf16[32,2,1024]{2,1,0:T(2,128)(2,1)}), bf16[32,2,1024]{2,1,0:T(2,128)(2,1)S(1)}, u32[]{:S(2)}, u32[]{:S(2)}) async-start(bf16[32,2,1024]{2,1,0:T(2,128)(2,1)} %reshape.1260), calls=%async_computation | async-start | bytes 262144 | tf_op jit(solution)/shard_map/all_to_all | solution.py:43
  172.3 29.0 %all-to-all-done = bf16[32,2,1024]{2,1,0:T(2,128)(2,1)S(1)} async-done(((bf16[32,2,1024]{2,1,0:T(2,128)(2,1)}), bf16[32,2,1024]{2,1,0:T(2,128)(2,1)S(1)}, u32[]{:S(2)}, u32[]{:S(2)}) %all-to-all-start) | async-done | bytes 131104 | tf_op jit(solution)/shard_map/all_to_all | solution.py:43
  202.1 6.5 all_to_all.30
  209.9 122.0 %while.65 = (s32[]{:T(128)}, f32[1,16,1024]{2,1,0:T(8,128)S(1)}, f32[1,16,1024]{2,1,0:T(8,128)S(1)}, bf16[1,2,16,2048]{3,2,1,0:T(8,128)(2,1)S(1)}, f32[1]{0:T(12...) while((s32[]{:T(128)}, f32[1,16,1024]{2,1,0:T(8,128)S(1)}, ...), condition=%wide.region_3.0_spmd.clone, body=%wide.region_2.0_spmd.clone.sunk | while | flops 17928200 | bytes 826570 | solution.py:127
  332.1 4.2 all_to_all.31
  337.1 4.8 all-to-all-start.3
  344.3 39.8 %collective-permute-done = bf16[1,2,16,1024]{3,2,1,0:T(8,128)(2,1)S(1)} collective-permute-done((bf16[1,2,16,1024]{3,2,1,0:T(8,128)(2,1)S(1)}, bf16[1,2,16,1024]{3,2,1,0:T(8,128)(2,1)S(1)}, u32[]{:S(2)}, u32[]{:S(2)}) %collective-permute-start) | collective-permute-done | bytes 65568 | tf_op jit(solution)/shard_map/ppermute | solution.py:24
  384.1 5.2 collective-permute-start.1
  389.4 3.7 collective-permute-done.1
  393.1 12.3 %collective-permute-start.2 = (bf16[1,2,64,1024]{3,2,1,0:T(8,128)(2,1)S(1)}, bf16[1,2,64,1024]{3,2,1,0:T(8,128)(2,1)S(1)}, u32[]{:S(2)}, u32[]{:S(2)}) collective-permute-start(bf16[1,2,64,1024]{3,2,1,0:T(8,128)(2,1)S(1)} %maximum_select_fusion.1), channel_id=1, source_target_pairs={{0,32},{32,0},{8,40},{40,8},{16,48},{48,16},{24,56},{56,24},{64,96... | collective-permute-start | bytes 786440 | tf_op jit(solution)/shard_map/ppermute | solution.py:24
  405.5 22.0 %collective-permute-done.2 = bf16[1,2,64,1024]{3,2,1,0:T(8,128)(2,1)S(1)} collective-permute-done((bf16[1,2,64,1024]{3,2,1,0:T(8,128)(2,1)S(1)}, bf16[1,2,64,1024]{3,2,1,0:T(8,128)(2,1)S(1)}, u32[]{:S(2)}, u32[]{:S(2)}) %collective-permute-start.2) | collective-permute-done | bytes 262176 | tf_op jit(solution)/shard_map/ppermute | solution.py:24
  435.9 3.7 collective-permute-done.4
  439.7 4.3 collective-permute-start.5
  444.1 4.9 collective-permute-done.5
  449.6 127.4 %while.66 = (s32[]{:T(128)}, f32[1,16,2048]{2,1,0:T(8,128)S(1)}, f32[1,16,2048]{2,1,0:T(8,128)S(1)}, bf16[1,16,1024]{2,1,0:T(8,128)(2,1)S(1)}, f32[1]{0:T(128)},...) while((s32[]{:T(128)}, f32[1,16,2048]{2,1,0:T(8,128)S(1)}, ...), condition=%wide.region_5.7_spmd.clone, body=%wide.region_4.6_spmd.clone.sunk | while | flops 35848328 | bytes 1100998 | solution.py:212
  466.0 3.6 fusion.229
  469.6 3.6 convolution_bitcast_fusion.20
  480.4 3.6 fusion.229
  494.7 3.6 fusion.229
  509.0 3.6 fusion.229
  512.6 3.6 convolution_bitcast_fusion.20
  523.3 3.6 fusion.229
  537.7 3.6 fusion.229
  552.0 3.6 fusion.229
  555.6 3.6 convolution_bitcast_fusion.20
  566.3 3.6 fusion.229
  569.9 3.6 convolution_bitcast_fusion.20
  579.3 22.9 %all-to-all-start.4 = ((bf16[32,2,1024]{2,1,0:T(2,128)(2,1)}), bf16[32,2,1024]{2,1,0:T(2,128)(2,1)S(1)}, u32[]{:S(2)}, u32[]{:S(2)}) async-start(bf16[32,2,1024]{2,1,0:T(2,128)(2,1)} %reshape.1264), calls=%async_computation.4 | async-start | bytes 262144 | tf_op jit(solution)/shard_map/all_to_all | solution.py:43
  602.2 25.9 %all-to-all-done.4 = bf16[32,2,1024]{2,1,0:T(2,128)(2,1)S(1)} async-done(((bf16[32,2,1024]{2,1,0:T(2,128)(2,1)}), bf16[32,2,1024]{2,1,0:T(2,128)(2,1)S(1)}, u32[]{:S(2)}, u32[]{:S(2)}) %all-to-all-start.4) | async-done | bytes 131104 | tf_op jit(solution)/shard_map/all_to_all | solution.py:43
  629.2 9.4 %all_to_all.32 = bf16[2,2,16384]{2,1,0:T(2,128)(2,1)S(1)} all-to-all(bf16[2,2,16384]{2,1,0:T(2,128)(2,1)S(1)} %reshape.1266), channel_id=1, replica_groups=mesh['parts'=2,'shot'=32,'freq'=4,'rep'=2] {'rep'}, dimensions={0} | all-to-all | bytes 262144 | tf_op jit(solution)/shard_map/all_to_all | solution.py:43
  639.2 116.0 %while.67 = (s32[]{:T(128)}, f32[1,32,2048]{2,1,0:T(8,128)S(1)}, f32[1,32,2048]{2,1,0:T(8,128)S(1)}, bf16[1,2,1024,32]{3,2,1,0:T(8,128)(2,1)S(1)}, f32[1]{0:T(12...) while((s32[]{:T(128)}, f32[1,32,2048]{2,1,0:T(8,128)S(1)}, ...), condition=%wide.region_7.9_spmd.clone, body=%wide.region_6.8_spmd.clone.sunk | while | flops 69599360 | bytes 2526398 | solution.py:243
  643.0 3.6 fusion.240
  650.2 3.6 fusion.239
  657.5 3.6 fusion.240
  664.7 3.6 fusion.239
  672.0 3.6 fusion.240
  679.2 3.6 fusion.239
  686.5 3.6 fusion.240
  693.6 3.6 fusion.239
  700.9 3.6 fusion.240
  708.1 3.6 fusion.239
  715.4 3.6 fusion.240
  722.6 3.6 fusion.239
  729.9 3.6 fusion.240
  737.1 3.6 fusion.239
  744.3 3.6 fusion.240
  751.5 3.6 fusion.239
  (352 shorter events, 395.8 us)
Async XLA Ops:
  1.0 0.7 copy-start
  126.0 75.3 %all-to-all-start = ((bf16[32,2,1024]{2,1,0:T(2,128)(2,1)}), bf16[32,2,1024]{2,1,0:T(2,128)(2,1)S(1)}, u32[]{:S(2)}, u32[]{:S(2)}) async-start(bf16[32,2,1024]{2,1,0:T(2,128)(2,1)} %reshape.1260), calls=%async_computation | async-start | bytes 262144 | tf_op jit(solution)/shard_map/all_to_all | solution.py:43
  209.2 0.7 copy-start.1
  337.1 90.5 %all-to-all-start.3 = ((bf16[32,2,1,2,16,128]{5,4,1,3,2,0:T(8,128)(2,1)}), bf16[32,2,1,2,16,128]{5,4,1,3,2,0:T(8,128)(2,1)S(1)}, u32[]{:S(2)}, u32[]{:S(2)}) async-start(bf16[32,2,1,2,16,128]{5,4,1,3,2,0:T(8,128)(2,1)} %copy.66), calls=%async_computation.3 | async-start | bytes 1048576 | tf_op jit(solution)/shard_map/all_to_all | solution.py:43
  341.9 42.2 %collective-permute-start = (bf16[1,2,16,1024]{3,2,1,0:T(8,128)(2,1)S(1)}, bf16[1,2,16,1024]{3,2,1,0:T(8,128)(2,1)S(1)}, u32[]{:S(2)}, u32[]{:S(2)}) collective-permute-start(bf16[1,2,16,1024]{3,2,1,0:T(8,128)(2,1)S(1)} %get-tuple-element.718), channel_id=1, source_target_pairs={{0,8},{8,0},{16,24},{24,16},{32,40},{40,32},{48,56},{56,48},{64,72... | collective-permute-start | bytes 196616 | tf_op jit(solution)/shard_map/ppermute | solution.py:24
  384.1 8.9 %collective-permute-start.1 = (bf16[1,2,32,1024]{3,2,1,0:T(8,128)(2,1)S(1)}, bf16[1,2,32,1024]{3,2,1,0:T(8,128)(2,1)S(1)}, u32[]{:S(2)}, u32[]{:S(2)}) collective-permute-start(bf16[1,2,32,1024]{3,2,1,0:T(8,128)(2,1)S(1)} %maximum_select_fusion.3), channel_id=1, source_target_pairs={{0,16},{16,0},{8,24},{24,8},{32,48},{48,32},{40,56},{56,40},{64,80... | collective-permute-start | bytes 393224 | tf_op jit(solution)/shard_map/ppermute | solution.py:24
  393.1 34.4 %collective-permute-start.2 = (bf16[1,2,64,1024]{3,2,1,0:T(8,128)(2,1)S(1)}, bf16[1,2,64,1024]{3,2,1,0:T(8,128)(2,1)S(1)}, u32[]{:S(2)}, u32[]{:S(2)}) collective-permute-start(bf16[1,2,64,1024]{3,2,1,0:T(8,128)(2,1)S(1)} %maximum_select_fusion.1), channel_id=1, source_target_pairs={{0,32},{32,0},{8,40},{40,8},{16,48},{48,16},{24,56},{56,24},{64,96... | collective-permute-start | bytes 786440 | tf_op jit(solution)/shard_map/ppermute | solution.py:24
  429.3 4.7 collective-permute-start.3
  434.0 5.7 collective-permute-start.4
  439.7 9.3 %collective-permute-start.5 = (bf16[1,2,1,4,16,128]{5,4,3,1,2,0:T(8,128)(2,1)S(1)}, bf16[1,2,1,4,16,128]{5,4,3,1,2,0:T(8,128)(2,1)S(1)}, u32[]{:S(2)}, u32[]{:S(2)}) collective-permute-start(bf16[1,2,1,4,16,128]{5,4,3,1,2,0:T(8,128)(2,1)S(1)} %get-tuple-element.709), channel_id=1, source_target_pairs={{0,32},{32,0},{8,40},{40,8},{16,48},{48,16},{24,56},{56,24},{64,96... | collective-permute-start | bytes 98312 | tf_op jit(solution)/shard_map/ppermute | solution.py:24
  579.3 48.7 %all-to-all-start.4 = ((bf16[32,2,1024]{2,1,0:T(2,128)(2,1)}), bf16[32,2,1024]{2,1,0:T(2,128)(2,1)S(1)}, u32[]{:S(2)}, u32[]{:S(2)}) async-start(bf16[32,2,1024]{2,1,0:T(2,128)(2,1)} %reshape.1264), calls=%async_computation.4 | async-start | bytes 262144 | tf_op jit(solution)/shard_map/all_to_all | solution.py:43
where the time goes:
time: 764 us; the launch traced here: 756 us
  matrix products  470 us (62%)
  waiting for transfers between devices  132 us (17%)
  starting transfers between devices  102 us (13%)
  blocking collectives  20.1 us (3%)
  local copies, waits for them, and re-layouts  14.1 us (2%)
  loops' own time  13.9 us (2%)
    dot_general x196, matrix products, contract_product(): return jnp.einsum(form, left, right, preferred_element_type=jnp.float32)  470 us
    ppermute x6, waiting for transfers between devices, from_partner(): return lax.ppermute(block, axis, route)  76.8 us
    all_to_all x3, starting transfers between devices, moved_by_axis(): lax.all_to_all(tiles, axes[k], split_axis=k, concat_axis=k, tiled=True)  74 us
    all_to_all x3, waiting for transfers between devices, moved_by_axis(): lax.all_to_all(tiles, axes[k], split_axis=k, concat_axis=k, tiled=True)  54.9 us
    ppermute x6, starting transfers between devices, from_partner(): return lax.ppermute(block, axis, route)  28.1 us
    all_to_all x3, blocking collectives, moved_by_axis(): lax.all_to_all(tiles, axes[k], split_axis=k, concat_axis=k, tiled=True)  20.1 us
  transfers between devices with their start and end apart: 9, of which 8 were waited for; matrix products, arithmetic and copies ran while one was open for 0% of the time, Pallas kernels for 0%

commit v1 on v0

v1 whole, which is shorter than its diff:
```python
import math

import jax
import jax.numpy as jnp
from jax import lax
from jax.experimental import pallas as pl
from jax.experimental.pallas import tpu as pltpu
from jax.sharding import Mesh
from jax.sharding import PartitionSpec as P

NSLOW = 1024
FINE = 8
NEAR = 4

two_pi = 6.283185307179586
base_hertz = 40.0
step_hertz = 0.5
slow_max = 0.0005

GROUP = ("far", "near", "rep")


def source_row(a, b):
    return (b * FINE + a) * 2 * FINE


def receiver_row(a, b):
    half = FINE // 2
    return ((a // half * FINE + b) * half + a % half) * 2 * FINE


def seed_slowness():
    rows = jnp.arange(3 * FINE, dtype=jnp.int32)
    level, index = rows // FINE, rows % FINE
    odd = jnp.where(level == 0, 2 * index + 1, jnp.where(level == 1, 2 * FINE * index, 2 * FINE * FINE * index))
    return slow_max * (odd.astype(jnp.float32) / NSLOW)


def seeds(omega, positions):
    phases = (omega * seed_slowness())[:, None] * positions[None, :]
    return jnp.cos(phases), jnp.sin(phases)


def fill_table(cos_ref, sin_ref, table_ref, row_of):
    width = min(256, table_ref.shape[1])

    def fill(step, carry):
        lanes = pl.ds(pl.multiple_of(step * width, width), width)
        c0, s0 = cos_ref[0:FINE, lanes], sin_ref[0:FINE, lanes]
        inner = [(c0, s0)]
        for b in range(1, FINE):
            cb, sb = cos_ref[pl.ds(FINE + b, 1), lanes], sin_ref[pl.ds(FINE + b, 1), lanes]
            inner.append((c0 * cb - s0 * sb, s0 * cb + c0 * sb))
        for a in range(FINE):
            ca, sa = cos_ref[pl.ds(2 * FINE + a, 1), lanes], sin_ref[pl.ds(2 * FINE + a, 1), lanes]
            for b, (c, s) in enumerate(inner):
                if a > 0:
                    c, s = c * ca - s * sa, s * ca + c * sa
                rows = jnp.concatenate([c, s], axis=0).astype(jnp.bfloat16)
                table_ref[pl.ds(row_of(a, b), 2 * FINE), lanes] = rows
        return carry

    lax.fori_loop(0, table_ref.shape[1] // width, fill, 0)


def dot_last(left, right):
    return lax.dot_general(left, right, (((1,), (1,)), ((), ())), preferred_element_type=jnp.float32)


def split_parts(x, scale):
    lanes = x.shape[1]
    x = (x * scale).reshape(2 * FINE, 2, FINE, lanes)
    return [x[:, part].reshape(2 * FINE * FINE, lanes) for part in range(2)]


def forward_kernel(data_ref, cos_ref, sin_ref, spread_ref, table_ref):
    fill_table(cos_ref, sin_ref, table_ref, receiver_row)
    total = dot_last(table_ref[...], data_ref[...]) * (1.0 / math.sqrt(data_ref.shape[1]))
    for a in range(FINE):
        for b in range(FINE):
            row = receiver_row(a, b)
            pair = [total[row : row + FINE], total[row + FINE : row + 2 * FINE]]
            spread_ref[a * FINE + b] = jnp.concatenate(pair, axis=1).astype(jnp.bfloat16)


def planes_kernel(gathered_ref, cos_ref, sin_ref, planes_ref, table_ref):
    peers, _, lanes = gathered_ref.shape
    shots = table_ref.shape[1] // peers
    fill_table(cos_ref, sin_ref, table_ref, source_row)
    got = gathered_ref[...].astype(jnp.float32)
    lines = []
    for kind in range(lanes // shots):
        pieces = [got[d, :, kind * shots : (kind + 1) * shots] for d in range(peers)]
        lines.append(jnp.concatenate(pieces, axis=1))
    stacked = jnp.concatenate(lines, axis=0).astype(jnp.bfloat16)
    total = dot_last(table_ref[...], stacked) * (1.0 / math.sqrt(table_ref.shape[1]))
    planes_ref[...] = total.T.astype(jnp.bfloat16)


def inner_kernel(planes_ref, cos_ref, sin_ref, inner_ref, table_ref):
    fill_table(cos_ref, sin_ref, table_ref, source_row)
    total = jnp.dot(planes_ref[...], table_ref[...], preferred_element_type=jnp.float32)
    both = jnp.concatenate(split_parts(total, 2.0 / math.sqrt(NSLOW)), axis=1)
    rows = lax.broadcasted_iota(jnp.int32, both.shape, 0)
    inner_ref[...] = jnp.where(rows // FINE % 2 == 0, both, -both).astype(jnp.bfloat16)


def back_kernel(rep_ref, planes_ref, mine_ref, other_ref, back_ref, inner_ref):
    rep = rep_ref[0]
    rows = 2 * FINE * FINE
    for near in range(NEAR):
        first = pl.multiple_of((2 * near + rep) * rows, rows)
        second = pl.multiple_of((2 * near + 1 - rep) * rows, rows)
        inner_ref[pl.ds(first, rows), :] = mine_ref[near * rows : (near + 1) * rows, :]
        inner_ref[pl.ds(second, rows), :] = other_ref[near * rows : (near + 1) * rows, :]
    total = jnp.dot(planes_ref[...], inner_ref[...], preferred_element_type=jnp.float32)
    upper, lower = split_parts(total, 2.0 / math.sqrt(NSLOW))
    shots = upper.shape[1] // 2
    real = upper[:, :shots] - lower[:, shots:]
    imaginary = lower[:, :shots] + upper[:, shots:]
    peers, half, lanes = back_ref.shape
    own = lanes // 4
    for peer in range(peers):
        span = slice(peer * own, (peer + 1) * own)
        pieces = [real[:half, span], imaginary[:half, span], real[half:, span], imaginary[half:, span]]
        back_ref[peer] = jnp.concatenate(pieces, axis=1).astype(jnp.bfloat16)


def inverse_kernel(back_ref, cos_ref, sin_ref, out_ref, table_ref):
    fill_table(cos_ref, sin_ref, table_ref, receiver_row)
    peers, half, lanes = back_ref.shape
    turned = back_ref[...].astype(jnp.float32).reshape(peers * half, lanes).T
    back = jnp.concatenate([turned[: lanes // 2], turned[lanes // 2 :]], axis=1).astype(jnp.bfloat16)
    total = jnp.dot(back, table_ref[...], preferred_element_type=jnp.float32)
    out_ref[...] = (total * (2.0 / math.sqrt(NSLOW))).astype(jnp.bfloat16)


def call(kernel, shape, scratch, *operands):
    spec = pl.BlockSpec(memory_space=pltpu.VMEM)
    scalar = pl.BlockSpec(memory_space=pltpu.SMEM)
    return pl.pallas_call(
        kernel,
        out_shape=jax.ShapeDtypeStruct(shape, jnp.bfloat16),
        in_specs=[scalar if x.dtype == jnp.int32 else spec for x in operands],
        out_specs=spec,
        scratch_shapes=[pltpu.VMEM(scratch, jnp.bfloat16)],
        compiler_params=pltpu.CompilerParams(vmem_limit_bytes=40 * 2**20),
    )(*operands)


def body(recorded, receiver_x, source_x):
    _, _, shots, receivers = recorded.shape
    sources = source_x.shape[0]
    near_peers = lax.axis_size("near") * lax.axis_size("rep")
    peers = lax.axis_size("far") * near_peers
    far, rep = lax.axis_index("far"), lax.axis_index("rep")
    omega = two_pi * (base_hertz + step_hertz * lax.axis_index("freq").astype(jnp.float32))
    data = recorded.reshape(2 * shots, receivers)

    receiver_seeds = seeds(omega, receiver_x)
    spread = call(forward_kernel, (peers, FINE, 4 * shots), (NSLOW, receivers), data, *receiver_seeds)
    gathered = lax.all_to_all(spread, GROUP, 0, 0, tiled=True)

    source_seeds = seeds(omega, source_x)
    planes = call(planes_kernel, (4 * FINE, NSLOW), (NSLOW, sources), gathered, *source_seeds)
    planes = lax.all_gather(planes, "far", axis=0, tiled=True)

    around = near_peers * shots
    around_seeds = [lax.dynamic_slice_in_dim(x, far * around, around, 1) for x in source_seeds]
    inner = call(inner_kernel, (2 * FINE * FINE, 2 * around), (NSLOW, around), planes, *around_seeds)
    mine = lax.all_gather(inner, "near", axis=0, tiled=True)
    other = lax.ppermute(mine, "rep", [(0, 1), (1, 0)])
    back = call(
        back_kernel,
        (near_peers, FINE * FINE, 4 * shots),
        (NSLOW, 2 * around),
        rep.astype(jnp.int32).reshape(1),
        planes,
        mine,
        other,
    )
    back = lax.all_to_all(back, ("near", "rep"), 0, 0, tiled=True)
    out = call(inverse_kernel, (2 * shots, receivers), (NSLOW, receivers), back, *receiver_seeds)
    return out.reshape(recorded.shape)


def solution(mesh):
    parts, shot, freq, rep = (mesh.shape[name] for name in ("parts", "shot", "freq", "rep"))
    devices = mesh.devices.reshape(parts, shot // NEAR, NEAR, freq, rep)
    split = Mesh(devices, ("parts", "far", "near", "freq", "rep"))
    placed = P(None, ("parts", "freq"), GROUP, None)
    return jax.shard_map(
        body,
        mesh=split,
        in_specs=(placed, P("parts"), P("parts")),
        out_specs=placed,
        check_vma=False,
    )
```

time: 764 us -> 161 us (0.21)
  matrix products: 470 us -> 0 us
  waiting for transfers between devices: 132 us -> 31.5 us
  starting transfers between devices: 102 us -> 61.4 us
  blocking collectives: 20.1 us -> 55.6 us
  loops' own time: 13.9 us -> 0 us
  local copies, waits for them, and re-layouts: 14.1 us -> 0.72 us
  Pallas kernels: 0 us -> 8.79 us
    dot_general x196 -> x0, matrix products: 470 us -> none  [contract_product(): return jnp.einsum(form, left, right, preferred_element_type=jnp.float32)]
    ppermute x6 -> x1, waiting for transfers between devices: 76.8 us -> 1.51 us  [body(): other = lax.ppermute(mine, 'rep', [(0, 1), (1, 0)])]
    all_gather x0 -> x2, blocking collectives: none -> 46.2 us  [the longest x1 33.9 us: body(): planes = lax.all_gather(planes, 'far', axis=0, tiled=True)]
    all_to_all x3 -> x1, starting transfers between devices: 74 us -> 47.4 us  [body(): gathered = lax.all_to_all(spread, GROUP, 0, 0, tiled=True)]
    all_to_all x3 -> x1, waiting for transfers between devices: 54.9 us -> 30 us  [body(): gathered = lax.all_to_all(spread, GROUP, 0, 0, tiled=True)]
    ppermute x6 -> x1, starting transfers between devices: 28.1 us -> 14 us  [body(): other = lax.ppermute(mine, 'rep', [(0, 1), (1, 0)])]
    another operation x4 -> x0, loops' own time: 13.9 us -> none  [the longest x1 12.8 us: source_inverse(): lax.fori_loop(0, slow_count // width_block, accumulate, (initial, initial))]
    all_to_all x3 -> x1, blocking collectives: 20.1 us -> 9.42 us  [body(): back = lax.all_to_all(back, ('near', 'rep'), 0, 0, tiled=True)]
  transfers between devices with their start and end apart: 9 -> 2, of which waited for: 8 -> 2; matrix products, arithmetic and copies ran while one was open for 0% -> 0% of each run, Pallas kernels for 0% -> 0%
where the time goes in v1:
time: 161 us; the launch traced here: 160 us
  starting transfers between devices  61.4 us (38%)
  blocking collectives  55.6 us (35%)
  waiting for transfers between devices  31.5 us (20%)
  Pallas kernels  8.79 us (5%)
    all_to_all x1, starting transfers between devices, body(): gathered = lax.all_to_all(spread, GROUP, 0, 0, tiled=True)  47.4 us
    all_gather x1, blocking collectives, body(): planes = lax.all_gather(planes, 'far', axis=0, tiled=True)  33.9 us
    all_to_all x1, waiting for transfers between devices, body(): gathered = lax.all_to_all(spread, GROUP, 0, 0, tiled=True)  30 us
    ppermute x1, starting transfers between devices, body(): other = lax.ppermute(mine, 'rep', [(0, 1), (1, 0)])  14 us
    all_gather x1, blocking collectives, body(): mine = lax.all_gather(inner, 'near', axis=0, tiled=True)  12.3 us
    all_to_all x1, blocking collectives, body(): back = lax.all_to_all(back, ('near', 'rep'), 0, 0, tiled=True)  9.42 us
    pallas_call x5, Pallas kernels, call(): pl.pallas_call(kernel, out_shape=jax.ShapeDtypeStruct(shape, jnp.bfloat16...  8.79 us
  transfers between devices with their start and end apart: 2, of which 2 were waited for; matrix products, arithmetic and copies ran while one was open for 0% of the time, Pallas kernels for 0%

profile of v1, /device:TPU:33, one launch (start us, length us, event | category | flops | bytes accessed | tf_op | source)
XLA Modules:
  0.0 159.5 jit_solution(7282660579717417159)
XLA Ops:
  0.0 0.0 copy-start.2
  0.0 0.0 copy-start.1
  0.0 0.7 copy-done.2
  0.7 0.0 copy-done.1
  0.7 0.0 copy-start
  0.7 1.4 multiply_sine_fusion
  2.2 0.0 copy-done
  2.2 2.9 %shard_map.37 = bf16[64,8,128]{2,1,0:T(8,128)(2,1)} custom-call(bf16[64,2048]{1,0:T(8,128)(2,1)S(1)} %bitcast.5, f32[24,2048]{1,0:T(8,128)S(1)} %get-tuple-element.9.cos_ref, f32[24,2048]{1,0:T(8,128)S(1)} %get-tuple-element.10.sin_ref), custom_call_target="tpu_custom_call" | custom-call | tf_op jit(solution)/shard_map/pallas_call | solution.py:141
  5.1 47.4 %all-to-all-start = ((bf16[64,8,128]{2,1,0:T(8,128)(2,1)}), bf16[64,8,128]{2,1,0:T(8,128)(2,1)S(1)}, u32[]{:S(2)}, u32[]{:S(2)}) async-start(bf16[64,8,128]{2,1,0:T(8,128)(2,1)} %shard_map.37), calls=%async_computation | async-start | bytes 262144 | tf_op jit(solution)/shard_map/all_to_all | solution.py:162
  52.6 30.0 %all-to-all-done.gathered_ref = bf16[64,8,128]{2,1,0:T(8,128)(2,1)S(1)} async-done(((bf16[64,8,128]{2,1,0:T(8,128)(2,1)}), bf16[64,8,128]{2,1,0:T(8,128)(2,1)S(1)}, u32[]{:S(2)}, u32[]{:S(2)}) %all-to-all-start) | async-done | bytes 131104 | tf_op jit(solution)/shard_map/all_to_all | solution.py:162
  82.6 2.3 %shard_map.38 = bf16[32,1024]{1,0:T(8,128)(2,1)S(1)} custom-call(bf16[64,8,128]{2,1,0:T(8,128)(2,1)S(1)} %all-to-all-done.gathered_ref, f32[24,2048]{1,0:T(8,128)S(1)} %get-tuple-element.6.cos_ref, f32[24,2048]{1,0:T(8,128)S(1)} %get-tuple-element.5.sin_ref), custom_call_target="tpu_custom_call" | custom-call | tf_op jit(solution)/shard_map/pallas_call | solution.py:141
  84.9 33.9 %all_gather.6.planes_ref = bf16[256,1024]{1,0:T(8,128)(2,1)S(1)} all-gather(bf16[32,1024]{1,0:T(8,128)(2,1)S(1)} %shard_map.38), channel_id=1, replica_groups=mesh['parts'=2,'far'=8,'near'=4,'freq'=4,'rep'=2] {'far'}, dimensions={0}, use_global_device_ids=true | all-gather | bytes 589824 | tf_op jit(solution)/shard_map/all_gather | solution.py:166
  118.8 0.3 shard_map.39
  119.2 12.3 %all_gather.7.mine_ref = bf16[512,512]{1,0:T(8,128)(2,1)S(1)} all-gather(bf16[128,512]{1,0:T(8,128)(2,1)S(1)} %shard_map.39), channel_id=1, replica_groups=mesh['parts'=2,'far'=8,'near'=4,'freq'=4,'rep'=2] {'near'}, dimensions={0}, use_global_device_ids=true | all-gather | bytes 655360 | tf_op jit(solution)/shard_map/all_gather | solution.py:171
  131.4 14.0 %collective-permute-start = (bf16[512,512]{1,0:T(8,128)(2,1)S(1)}, bf16[512,512]{1,0:T(8,128)(2,1)S(1)}, u32[]{:S(2)}, u32[]{:S(2)}) collective-permute-start(bf16[512,512]{1,0:T(8,128)(2,1)S(1)} %all_gather.7.mine_ref), channel_id=1, source_target_pairs={{0,1},{1,0},{2,3},{3,2},{4,5},{5,4},{6,7},{7,6},{8,9},{9,8},{10,11... | collective-permute-start | bytes 1572872 | tf_op jit(solution)/shard_map/ppermute | solution.py:172
  145.4 1.5 collective-permute-done.other_ref
  146.9 0.6 shard_map.40
  147.5 9.4 %all_to_all.10.back_ref = bf16[8,64,128]{2,1,0:T(8,128)(2,1)S(1)} all-to-all(bf16[8,64,128]{2,1,0:T(8,128)(2,1)S(1)} %shard_map.40), channel_id=1, replica_groups=mesh['parts'=2,'far'=8,'near'=4,'freq'=4,'rep'=2] {'near','rep'}, dimensions={0} | all-to-all | bytes 262144 | tf_op jit(solution)/shard_map/all_to_all | solution.py:182
  156.9 2.6 %shard_map.41 = bf16[64,2048]{1,0:T(8,128)(2,1)} custom-call(bf16[8,64,128]{2,1,0:T(8,128)(2,1)S(1)} %all_to_all.10.back_ref, f32[24,2048]{1,0:T(8,128)S(1)} %get-tuple-element.9.cos_ref, f32[24,2048]{1,0:T(8,128)S(1)} %get-tuple-element.10.sin_ref), custom_call_target="tpu_custom_call" | custom-call | tf_op jit(solution)/shard_map/pallas_call | solution.py:141
  (2 shorter events, 0.0 us)
Async XLA Ops:
  0.0 0.7 copy-start.2
  0.0 0.7 copy-start.1
  0.7 1.4 copy-start
  5.1 77.5 %all-to-all-start = ((bf16[64,8,128]{2,1,0:T(8,128)(2,1)}), bf16[64,8,128]{2,1,0:T(8,128)(2,1)S(1)}, u32[]{:S(2)}, u32[]{:S(2)}) async-start(bf16[64,8,128]{2,1,0:T(8,128)(2,1)} %shard_map.37), calls=%async_computation | async-start | bytes 262144 | tf_op jit(solution)/shard_map/all_to_all | solution.py:162
  131.4 15.5 %collective-permute-start = (bf16[512,512]{1,0:T(8,128)(2,1)S(1)}, bf16[512,512]{1,0:T(8,128)(2,1)S(1)}, u32[]{:S(2)}, u32[]{:S(2)}) collective-permute-start(bf16[512,512]{1,0:T(8,128)(2,1)S(1)} %all_gather.7.mine_ref), channel_id=1, source_target_pairs={{0,1},{1,0},{2,3},{3,2},{4,5},{5,4},{6,7},{7,6},{8,9},{9,8},{10,11... | collective-permute-start | bytes 1572872 | tf_op jit(solution)/shard_map/ppermute | solution.py:172

commit v2 on v1

v2 whole, which is shorter than its diff:
```python
import math

import jax
import jax.numpy as jnp
from jax import lax
from jax.experimental import pallas as pl
from jax.experimental.pallas import tpu as pltpu
from jax.sharding import Mesh
from jax.sharding import PartitionSpec as P

NSLOW = 1024
FINE = 8
NEAR = 4

two_pi = 6.283185307179586
base_hertz = 40.0
step_hertz = 0.5
slow_max = 0.0005

GROUP = ("far", "near", "rep")


def source_row(kind, a, b):
    return ((b * 2 + kind) * FINE + a) * FINE


def receiver_row(kind, a, b):
    return ((kind * FINE + b) * FINE + a) * FINE


def seed_slowness():
    rows = jnp.arange(3 * FINE, dtype=jnp.int32)
    level, index = rows // FINE, rows % FINE
    odd = jnp.where(level == 0, 2 * index + 1, jnp.where(level == 1, 2 * FINE * index, 2 * FINE * FINE * index))
    return slow_max * (odd.astype(jnp.float32) / NSLOW)


def seeds(omega, positions):
    phases = (omega * seed_slowness())[:, None] * positions[None, :]
    return jnp.cos(phases), jnp.sin(phases)


def fill_table(cos_ref, sin_ref, table_ref, row_of):
    width = min(256, table_ref.shape[1])

    def fill(step, carry):
        lanes = pl.ds(pl.multiple_of(step * width, width), width)
        c0, s0 = cos_ref[0:FINE, lanes], sin_ref[0:FINE, lanes]
        inner = [(c0, s0)]
        for b in range(1, FINE):
            cb, sb = cos_ref[pl.ds(FINE + b, 1), lanes], sin_ref[pl.ds(FINE + b, 1), lanes]
            inner.append((c0 * cb - s0 * sb, s0 * cb + c0 * sb))
        for a in range(0, FINE, 2):
            turns = [
                (cos_ref[pl.ds(2 * FINE + k, 1), lanes], sin_ref[pl.ds(2 * FINE + k, 1), lanes]) for k in (a, a + 1)
            ]
            for b, (c, s) in enumerate(inner):
                pairs = [(c * ca - s * sa, s * ca + c * sa) for ca, sa in turns]
                for kind in range(2):
                    rows = jnp.concatenate([pair[kind] for pair in pairs], axis=0).astype(jnp.bfloat16)
                    table_ref[pl.ds(row_of(kind, a, b), 2 * FINE), lanes] = rows
        return carry

    lax.fori_loop(0, table_ref.shape[1] // width, fill, 0)


def dot_last(left, right):
    return lax.dot_general(left, right, (((1,), (1,)), ((), ())), preferred_element_type=jnp.float32)


def split_parts(x, scale):
    rows, lanes = x.shape
    x = (x * scale).reshape(2, 2, rows // 4, lanes)
    return [x[:, part].reshape(rows // 2, lanes) for part in range(2)]


def forward_kernel(data_ref, cos_ref, sin_ref, spread_ref, table_ref):
    fill_table(cos_ref, sin_ref, table_ref, receiver_row)
    total = dot_last(table_ref[...], data_ref[...]) * (1.0 / math.sqrt(data_ref.shape[1]))
    half = total.shape[0] // 2
    both = jnp.concatenate([total[:half], total[half:]], axis=1)
    spread_ref[...] = both.reshape(spread_ref.shape).astype(jnp.bfloat16)


def turn_kernel(near_ref, main_ref, rest_ref):
    peers, rows, lanes = near_ref.shape
    shots = lanes // 4
    got = near_ref[...].astype(jnp.float32)
    lines = []
    for kind in range(4):
        pieces = [got[d, :, kind * shots : (kind + 1) * shots] for d in range(peers)]
        lines.append(jnp.concatenate(pieces, axis=1))
    turned = jnp.concatenate(lines, axis=0).astype(jnp.bfloat16)
    main = main_ref.shape[0]
    main_ref[...] = turned[:main]
    for far in range(rest_ref.shape[0]):
        rest_ref[far] = turned[main:]


def planes_kernel(far_ref, main_ref, rest_ref, cos_ref, sin_ref, planes_ref, inner_ref, table_ref, spread_ref):
    fill_table(cos_ref, sin_ref, table_ref, source_row)
    peers, main, around = main_ref.shape
    for far in range(peers):
        spread_ref[:main, far * around : (far + 1) * around] = main_ref[far]
        spread_ref[main:, far * around : (far + 1) * around] = rest_ref[far]
    total = dot_last(table_ref[...], spread_ref[...]) * (1.0 / math.sqrt(table_ref.shape[1]))
    planes = total.T.astype(jnp.bfloat16)
    planes_ref[...] = planes
    own = table_ref[:, pl.ds(pl.multiple_of(far_ref[0] * around, around), around)]
    total = jnp.dot(planes, own, preferred_element_type=jnp.float32)
    both = jnp.concatenate(split_parts(total, 2.0 / math.sqrt(NSLOW)), axis=1)
    half = both.shape[0] // 2
    inner_ref[:half] = both[:half].astype(jnp.bfloat16)
    inner_ref[half:] = (-both[half:]).astype(jnp.bfloat16)


def back_kernel(rep_ref, planes_ref, mine_ref, other_ref, back_ref, inner_ref):
    rep = rep_ref[0]
    rows = 2 * FINE * FINE
    for near in range(NEAR):
        first = pl.multiple_of((2 * near + rep) * rows, rows)
        second = pl.multiple_of((2 * near + 1 - rep) * rows, rows)
        inner_ref[pl.ds(first, rows), :] = mine_ref[near * rows : (near + 1) * rows, :]
        inner_ref[pl.ds(second, rows), :] = other_ref[near * rows : (near + 1) * rows, :]
    total = jnp.dot(planes_ref[...], inner_ref[...], preferred_element_type=jnp.float32)
    upper, lower = split_parts(total, 2.0 / math.sqrt(NSLOW))
    shots = upper.shape[1] // 2
    real = upper[:, :shots] - lower[:, shots:]
    imaginary = lower[:, :shots] + upper[:, shots:]
    peers, half, lanes = back_ref.shape
    own = lanes // 4
    for peer in range(peers):
        span = slice(peer * own, (peer + 1) * own)
        pieces = [real[:half, span], imaginary[:half, span], real[half:, span], imaginary[half:, span]]
        back_ref[peer] = jnp.concatenate(pieces, axis=1).astype(jnp.bfloat16)


def inverse_kernel(back_ref, cos_ref, sin_ref, out_ref, table_ref):
    fill_table(cos_ref, sin_ref, table_ref, receiver_row)
    peers, half, lanes = back_ref.shape
    turned = back_ref[...].astype(jnp.float32).reshape(peers * half, lanes).T
    back = jnp.concatenate([turned[: lanes // 2], turned[lanes // 2 :]], axis=1).astype(jnp.bfloat16)
    total = jnp.dot(back, table_ref[...], preferred_element_type=jnp.float32)
    out_ref[...] = (total * (2.0 / math.sqrt(NSLOW))).astype(jnp.bfloat16)


def call(kernel, shapes, scratch, *operands):
    spec = pl.BlockSpec(memory_space=pltpu.VMEM)
    scalar = pl.BlockSpec(memory_space=pltpu.SMEM)
    return pl.pallas_call(
        kernel,
        out_shape=[jax.ShapeDtypeStruct(shape, jnp.bfloat16) for shape in shapes],
        in_specs=[scalar if x.dtype == jnp.int32 else spec for x in operands],
        out_specs=[spec] * len(shapes),
        scratch_shapes=[pltpu.VMEM(shape, jnp.bfloat16) for shape in scratch],
        compiler_params=pltpu.CompilerParams(vmem_limit_bytes=40 * 2**20),
    )(*operands)


def body(recorded, receiver_x, source_x):
    _, _, shots, receivers = recorded.shape
    sources = source_x.shape[0]
    near = ("near", "rep")
    peers = lax.axis_size("near") * lax.axis_size("rep")
    around = peers * shots
    far_peers = lax.axis_size("far")
    far, rep = [lax.axis_index(name).astype(jnp.int32).reshape(1) for name in ("far", "rep")]
    omega = two_pi * (base_hertz + step_hertz * lax.axis_index("freq").astype(jnp.float32))
    data = recorded.reshape(2 * shots, receivers)
    receiver_seeds = seeds(omega, receiver_x)
    source_seeds = seeds(omega, source_x)
    receiver_table, source_table = (NSLOW, receivers), (NSLOW, sources)
    columns = 2 * NSLOW // peers
    rest = columns // 16
    chunk = (peers, FINE * FINE, 4 * shots)

    (spread,) = call(forward_kernel, [chunk], [receiver_table], data, *receiver_seeds)
    spread = lax.all_to_all(spread, near, 0, 0, tiled=True)
    most, last = call(turn_kernel, [(columns - rest, around), (far_peers, rest, around)], [], spread)
    last = lax.all_to_all(last, "far", 0, 0, tiled=True)
    most = lax.all_gather(most, "far", axis=0, tiled=False)
    planes, inner = call(
        planes_kernel,
        [(columns, NSLOW), (columns // 2, 2 * around)],
        [source_table, (columns, sources)],
        far,
        most,
        last,
        *source_seeds,
    )
    mine = lax.all_gather(inner, "near", axis=0, tiled=True)
    other = lax.ppermute(mine, "rep", [(0, 1), (1, 0)])
    (back,) = call(back_kernel, [chunk], [(NSLOW, 2 * around)], rep, planes, mine, other)
    back = lax.all_to_all(back, near, 0, 0, tiled=True)
    (out,) = call(inverse_kernel, [(2 * shots, receivers)], [receiver_table], back, *receiver_seeds)
    return out.reshape(recorded.shape)


def solution(mesh):
    parts, shot, freq, rep = (mesh.shape[name] for name in ("parts", "shot", "freq", "rep"))
    devices = mesh.devices.reshape(parts, shot // NEAR, NEAR, freq, rep)
    split = Mesh(devices, ("parts", "far", "near", "freq", "rep"))
    placed = P(None, ("parts", "freq"), GROUP, None)
    return jax.shard_map(
        body,
        mesh=split,
        in_specs=(placed, P("parts"), P("parts")),
        out_specs=placed,
        check_vma=False,
    )
```

time: 161 us -> 160 us (level)
  blocking collectives: 55.6 us -> 134 us
  starting transfers between devices: 61.4 us -> 12.8 us
  waiting for transfers between devices: 31.5 us -> 1.51 us
    all_to_all x1 -> x2, blocking collectives: 9.42 us -> 59.1 us  [the longest x1 49.7 us: body(): spread = lax.all_to_all(spread, near, 0, 0, tiled=True)]
    all_to_all x1, starting transfers between devices: 47.4 us -> 6.24 us  [body(): last = lax.all_to_all(last, 'far', 0, 0, tiled=True)]
    all_to_all x1, waiting for transfers between devices: 30 us -> 0.01 us  [body(): last = lax.all_to_all(last, 'far', 0, 0, tiled=True)]
    all_gather x1, blocking collectives: 33.9 us -> 60.6 us  [body(): most = lax.all_gather(most, 'far', axis=0, tiled=False)]
    ppermute x1, starting transfers between devices: 14 us -> 6.59 us  [body(): other = lax.ppermute(mine, 'rep', [(0, 1), (1, 0)])]
    all_gather x1, blocking collectives: 12.3 us -> 13.9 us  [body(): mine = lax.all_gather(inner, 'near', axis=0, tiled=True)]
  transfers between devices with their start and end apart: 2 -> 2, of which waited for: 2 -> 1; matrix products, arithmetic and copies ran while one was open for 0% -> 0% of each run, Pallas kernels for 0% -> 0%
where the time goes in v2:
time: 160 us; the launch traced here: 159 us
  blocking collectives  134 us (84%)
  starting transfers between devices  12.8 us (8%)
  Pallas kernels  9.23 us (6%)
    all_gather x1, blocking collectives, body(): most = lax.all_gather(most, 'far', axis=0, tiled=False)  60.6 us
    all_to_all x1, blocking collectives, body(): spread = lax.all_to_all(spread, near, 0, 0, tiled=True)  49.7 us
    all_gather x1, blocking collectives, body(): mine = lax.all_gather(inner, 'near', axis=0, tiled=True)  13.9 us
    all_to_all x1, blocking collectives, body(): back = lax.all_to_all(back, near, 0, 0, tiled=True)  9.37 us
    pallas_call x5, Pallas kernels, call(): pl.pallas_call(kernel, out_shape=[jax.ShapeDtypeStruct(shape, jnp.bfloat1...  9.23 us
    ppermute x1, starting transfers between devices, body(): other = lax.ppermute(mine, 'rep', [(0, 1), (1, 0)])  6.59 us
    all_to_all x1, starting transfers between devices, body(): last = lax.all_to_all(last, 'far', 0, 0, tiled=True)  6.24 us
  transfers between devices with their start and end apart: 2, of which 1 were waited for; matrix products, arithmetic and copies ran while one was open for 0% of the time, Pallas kernels for 0%

profile of v2, /device:TPU:33, one launch (start us, length us, event | category | flops | bytes accessed | tf_op | source)
XLA Modules:
  0.0 159.4 jit_solution(5566230229203753527)
XLA Ops:
  0.0 0.0 copy-start.2
  0.0 0.0 copy-start.1
  0.0 0.7 copy-done.2
  0.7 0.0 copy-done.1
  0.7 0.0 copy-start
  0.7 1.4 multiply_sine_fusion
  2.2 0.0 copy-done
  2.2 2.4 %shard_map.37 = bf16[8,64,128]{2,1,0:T(8,128)(2,1)S(1)} custom-call(bf16[64,2048]{1,0:T(8,128)(2,1)S(1)} %bitcast.8, f32[24,2048]{1,0:T(8,128)S(1)} %get-tuple-element.17.cos_ref, f32[24,2048]{1,0:T(8,128)S(1)} %get-tuple-element.18.sin_ref), custom_call_target="tpu_custom_call" | custom-call | tf_op jit(solution)/shard_map/pallas_call | solution.py:150
  4.6 49.7 %all_to_all.15.near_ref = bf16[8,64,128]{2,1,0:T(8,128)(2,1)S(1)} all-to-all(bf16[8,64,128]{2,1,0:T(8,128)(2,1)S(1)} %shard_map.37), channel_id=1, replica_groups=mesh['parts'=2,'far'=8,'near'=4,'freq'=4,'rep'=2] {'near','rep'}, dimensions={0} | all-to-all | bytes 262144 | tf_op jit(solution)/shard_map/all_to_all | solution.py:178
  54.3 0.8 shard_map.38
  55.1 6.2 %all-to-all-start.1 = ((bf16[8,16,256]{2,1,0:T(8,128)(2,1)}), bf16[8,16,256]{2,1,0:T(8,128)(2,1)S(1)}, u32[]{:S(2)}, u32[]{:S(2)}) async-start(bf16[8,16,256]{2,1,0:T(8,128)(2,1)} %get-tuple-element.10), calls=%async_computation.1 | async-start | bytes 131072 | tf_op jit(solution)/shard_map/all_to_all | solution.py:180
  61.3 60.6 %all-gather = bf16[1920,256]{1,0:T(8,128)(2,1)S(1)} all-gather(bf16[240,256]{1,0:T(8,128)(2,1)S(1)} %get-tuple-element.9), channel_id=2, replica_groups=mesh['parts'=2,'far'=8,'near'=4,'freq'=4,'rep'=2] {'far'}, dimensions={0}, use_global_device_ids=true | all-gather | bytes 1105920 | tf_op jit(solution)/shard_map/all_gather | solution.py:181
  121.9 0.0 all-to-all-done.1.rest_ref
  121.9 2.7 %shard_map.39 = (bf16[256,1024]{1,0:T(8,128)(2,1)S(1)}, bf16[128,512]{1,0:T(8,128)(2,1)S(1)}) custom-call(s32[1]{0:T(128)} %bitcast.1.far_ref, bf16[8,240,256]{2,1,0:T(8,128)(2,1)S(1)} %bitcast.7, bf16[8,16,256]{2,1,0:T(8,128)(2,1)S(1)} %all-to-all-done.1.rest_ref, f32[24,2048]{1,0:T(8,128)S(1)} %get-tuple-element.14.cos_ref, ...), custom_call_target="tpu_custom_call" | custom-call | tf_op jit(solution)/shard_map/pallas_call | solution.py:150
  124.7 13.9 %all_gather.11.mine_ref = bf16[512,512]{1,0:T(8,128)(2,1)S(1)} all-gather(bf16[128,512]{1,0:T(8,128)(2,1)S(1)} %get-tuple-element.12), channel_id=1, replica_groups=mesh['parts'=2,'far'=8,'near'=4,'freq'=4,'rep'=2] {'near'}, dimensions={0}, use_global_device_ids=true | all-gather | bytes 655360 | tf_op jit(solution)/shard_map/all_gather | solution.py:191
  138.6 6.6 %collective-permute-start = (bf16[512,512]{1,0:T(8,128)(2,1)S(1)}, bf16[512,512]{1,0:T(8,128)(2,1)S(1)}, u32[]{:S(2)}, u32[]{:S(2)}) collective-permute-start(bf16[512,512]{1,0:T(8,128)(2,1)S(1)} %all_gather.11.mine_ref), channel_id=1, source_target_pairs={{0,1},{1,0},{2,3},{3,2},{4,5},{5,4},{6,7},{7,6},{8,9},{9,8},{10,11... | collective-permute-start | bytes 1572872 | tf_op jit(solution)/shard_map/ppermute | solution.py:192
  145.2 1.5 collective-permute-done.other_ref
  146.7 0.6 shard_map.40
  147.3 9.4 %all_to_all.16.back_ref = bf16[8,64,128]{2,1,0:T(8,128)(2,1)S(1)} all-to-all(bf16[8,64,128]{2,1,0:T(8,128)(2,1)S(1)} %shard_map.40), channel_id=1, replica_groups=mesh['parts'=2,'far'=8,'near'=4,'freq'=4,'rep'=2] {'near','rep'}, dimensions={0} | all-to-all | bytes 262144 | tf_op jit(solution)/shard_map/all_to_all | solution.py:194
  156.7 2.7 %shard_map.41 = bf16[64,2048]{1,0:T(8,128)(2,1)} custom-call(bf16[8,64,128]{2,1,0:T(8,128)(2,1)S(1)} %all_to_all.16.back_ref, f32[24,2048]{1,0:T(8,128)S(1)} %get-tuple-element.17.cos_ref, f32[24,2048]{1,0:T(8,128)S(1)} %get-tuple-element.18.sin_ref), custom_call_target="tpu_custom_call" | custom-call | tf_op jit(solution)/shard_map/pallas_call | solution.py:150
  (1 shorter events, 0.0 us)
Async XLA Ops:
  0.0 0.7 copy-start.2
  0.0 0.7 copy-start.1
  0.7 1.4 copy-start
  55.1 66.9 %all-to-all-start.1 = ((bf16[8,16,256]{2,1,0:T(8,128)(2,1)}), bf16[8,16,256]{2,1,0:T(8,128)(2,1)S(1)}, u32[]{:S(2)}, u32[]{:S(2)}) async-start(bf16[8,16,256]{2,1,0:T(8,128)(2,1)} %get-tuple-element.10), calls=%async_computation.1 | async-start | bytes 131072 | tf_op jit(solution)/shard_map/all_to_all | solution.py:180
  138.6 8.1 %collective-permute-start = (bf16[512,512]{1,0:T(8,128)(2,1)S(1)}, bf16[512,512]{1,0:T(8,128)(2,1)S(1)}, u32[]{:S(2)}, u32[]{:S(2)}) collective-permute-start(bf16[512,512]{1,0:T(8,128)(2,1)S(1)} %all_gather.11.mine_ref), channel_id=1, source_target_pairs={{0,1},{1,0},{2,3},{3,2},{4,5},{5,4},{6,7},{7,6},{8,9},{9,8},{10,11... | collective-permute-start | bytes 1572872 | tf_op jit(solution)/shard_map/ppermute | solution.py:192

commit v3 on v2

--- a/solution.py
+++ b/solution.py
@@ -82,7 +82,11 @@
     spread_ref[...] = both.reshape(spread_ref.shape).astype(jnp.bfloat16)
 
 
-def turn_kernel(near_ref, main_ref, rest_ref):
+LEVEL = 13.0
+LEAST = 2.0**-100
+
+
+def turn_kernel(near_ref, turned_ref):
     peers, rows, lanes = near_ref.shape
     shots = lanes // 4
     got = near_ref[...].astype(jnp.float32)
@@ -90,19 +94,23 @@
     for kind in range(4):
         pieces = [got[d, :, kind * shots : (kind + 1) * shots] for d in range(peers)]
         lines.append(jnp.concatenate(pieces, axis=1))
-    turned = jnp.concatenate(lines, axis=0).astype(jnp.bfloat16)
-    main = main_ref.shape[0]
-    main_ref[...] = turned[:main]
-    for far in range(rest_ref.shape[0]):
-        rest_ref[far] = turned[main:]
-
-
-def planes_kernel(far_ref, main_ref, rest_ref, cos_ref, sin_ref, planes_ref, inner_ref, table_ref, spread_ref):
+    turned = jnp.concatenate(lines, axis=0)
+    largest = jnp.maximum(jnp.max(jnp.abs(turned), keepdims=True), LEAST)
+    exponent = jnp.ceil(jnp.log2(largest))
+    main = 4 * rows
+    turned_ref[:main] = (turned * jnp.exp2(LEVEL - exponent)).astype(turned_ref.dtype)
+    tail = jnp.broadcast_to(exponent, (turned_ref.shape[0] - main, turned.shape[1]))
+    turned_ref[main:] = tail.astype(turned_ref.dtype)
+
+
+def planes_kernel(far_ref, turned_ref, cos_ref, sin_ref, planes_ref, inner_ref, table_ref, spread_ref):
     fill_table(cos_ref, sin_ref, table_ref, source_row)
-    peers, main, around = main_ref.shape
+    peers, _, around = turned_ref.shape
+    main = spread_ref.shape[0]
     for far in range(peers):
-        spread_ref[:main, far * around : (far + 1) * around] = main_ref[far]
-        spread_ref[main:, far * around : (far + 1) * around] = rest_ref[far]
+        block = turned_ref[far].astype(jnp.float32)
+        block = block[:main] * jnp.exp2(block[main : main + 1, :1] - LEVEL)
+        spread_ref[:, far * around : (far + 1) * around] = block.astype(jnp.bfloat16)
     total = dot_last(table_ref[...], spread_ref[...]) * (1.0 / math.sqrt(table_ref.shape[1]))
     planes = total.T.astype(jnp.bfloat16)
     planes_ref[...] = planes
@@ -144,12 +152,12 @@
     out_ref[...] = (total * (2.0 / math.sqrt(NSLOW))).astype(jnp.bfloat16)
 
 
-def call(kernel, shapes, scratch, *operands):
+def call(kernel, shapes, scratch, *operands, dtype=jnp.bfloat16):
     spec = pl.BlockSpec(memory_space=pltpu.VMEM)
     scalar = pl.BlockSpec(memory_space=pltpu.SMEM)
     return pl.pallas_call(
         kernel,
-        out_shape=[jax.ShapeDtypeStruct(shape, jnp.bfloat16) for shape in shapes],
+        out_shape=[jax.ShapeDtypeStruct(shape, dtype) for shape in shapes],
         in_specs=[scalar if x.dtype == jnp.int32 else spec for x in operands],
         out_specs=[spec] * len(shapes),
         scratch_shapes=[pltpu.VMEM(shape, jnp.bfloat16) for shape in scratch],
@@ -163,7 +171,6 @@
     near = ("near", "rep")
     peers = lax.axis_size("near") * lax.axis_size("rep")
     around = peers * shots
-    far_peers = lax.axis_size("far")
     far, rep = [lax.axis_index(name).astype(jnp.int32).reshape(1) for name in ("far", "rep")]
     omega = two_pi * (base_hertz + step_hertz * lax.axis_index("freq").astype(jnp.float32))
     data = recorded.reshape(2 * shots, receivers)
@@ -171,21 +178,18 @@
     source_seeds = seeds(omega, source_x)
     receiver_table, source_table = (NSLOW, receivers), (NSLOW, sources)
     columns = 2 * NSLOW // peers
-    rest = columns // 16
     chunk = (peers, FINE * FINE, 4 * shots)
 
     (spread,) = call(forward_kernel, [chunk], [receiver_table], data, *receiver_seeds)
     spread = lax.all_to_all(spread, near, 0, 0, tiled=True)
-    most, last = call(turn_kernel, [(columns - rest, around), (far_peers, rest, around)], [], spread)
-    last = lax.all_to_all(last, "far", 0, 0, tiled=True)
-    most = lax.all_gather(most, "far", axis=0, tiled=False)
+    (turned,) = call(turn_kernel, [(columns + FINE, around)], [], spread, dtype=jnp.float32)
+    turned = lax.all_gather(turned.astype(jnp.float16), "far", axis=0, tiled=False).astype(jnp.float32)
     planes, inner = call(
         planes_kernel,
         [(columns, NSLOW), (columns // 2, 2 * around)],
         [source_table, (columns, sources)],
         far,
-        most,
-        last,
+        turned,
         *source_seeds,
     )
     mine = lax.all_gather(inner, "near", axis=0, tiled=True)

time: 160 us -> 153 us (0.956)
  the two profiles are of different devices: /device:TPU:33 before, /device:TPU:42 now
where the time goes in v3:
time: 153 us; the launch traced here: 152 us
  blocking collectives  121 us (79%)
  starting transfers between devices  10.4 us (7%)
  Pallas kernels  9.47 us (6%)
  waiting for transfers between devices  8.62 us (6%)
  other arithmetic  2.34 us (2%)
    all_gather x1, blocking collectives, body(): lax.all_gather(turned.astype(jnp.float16), 'far', axis=0, tiled=False)  95.4 us
    all_gather x1, blocking collectives, body(): mine = lax.all_gather(inner, 'near', axis=0, tiled=True)  15.9 us
    pallas_call x5, Pallas kernels, call(): pl.pallas_call(kernel, out_shape=[jax.ShapeDtypeStruct(shape, dtype) for...  9.47 us
    all_to_all x1, blocking collectives, body(): back = lax.all_to_all(back, near, 0, 0, tiled=True)  9.24 us
    all_to_all x1, starting transfers between devices, body(): spread = lax.all_to_all(spread, near, 0, 0, tiled=True)  8.49 us
    all_to_all x1, waiting for transfers between devices, body(): spread = lax.all_to_all(spread, near, 0, 0, tiled=True)  6.75 us
  transfers between devices with their start and end apart: 2, of which 2 were waited for; matrix products, arithmetic and copies ran while one was open for 0% of the time, Pallas kernels for 0%

profile of v3, /device:TPU:42, one launch (start us, length us, event | category | flops | bytes accessed | tf_op | source)
XLA Modules:
  0.0 152.5 jit_solution(8137385995918245486)
XLA Ops:
  0.0 2.1 %multiply_sine_fusion = (f32[24,2048]{1,0:T(8,128)S(1)}, f32[24,2048]{1,0:T(8,128)S(1)}, f32[24,2048]{1,0:T(8,128)S(1)}, f32[24,2048]{1,0:T(8,128)S(1)}) fusion(f32[2048]{0:T(1024)} %param.5, f32[24]{0:T(128)S(1)} %fusion.1, f32[2048]{0:T(1024)} %param.4), kind=kLoop, calls=%fused_computation | loop fusion | flops 98304 | bytes 802912 | tf_op jit(solution)/shard_map/sin | solution.py:40
  2.2 0.0 copy-start
  2.2 0.9 copy-done
  3.1 3.0 %shard_map.37 = bf16[8,64,128]{2,1,0:T(8,128)(2,1)} custom-call(bf16[64,2048]{1,0:T(8,128)(2,1)S(1)} %bitcast.8, f32[24,2048]{1,0:T(8,128)S(1)} %get-tuple-element.13.cos_ref, f32[24,2048]{1,0:T(8,128)S(1)} %get-tuple-element.14.sin_ref), custom_call_target="tpu_custom_call" | custom-call | tf_op jit(solution)/shard_map/pallas_call | solution.py:158
  6.2 8.5 %all-to-all-start = ((bf16[8,64,128]{2,1,0:T(8,128)(2,1)}), bf16[8,64,128]{2,1,0:T(8,128)(2,1)S(1)}, u32[]{:S(2)}, u32[]{:S(2)}) async-start(bf16[8,64,128]{2,1,0:T(8,128)(2,1)} %shard_map.37), calls=%async_computation | async-start | bytes 262144 | tf_op jit(solution)/shard_map/all_to_all | solution.py:184
  14.7 6.7 %all-to-all-done.near_ref = bf16[8,64,128]{2,1,0:T(8,128)(2,1)S(1)} async-done(((bf16[8,64,128]{2,1,0:T(8,128)(2,1)}), bf16[8,64,128]{2,1,0:T(8,128)(2,1)S(1)}, u32[]{:S(2)}, u32[]{:S(2)}) %all-to-all-start) | async-done | bytes 131104 | tf_op jit(solution)/shard_map/all_to_all | solution.py:184
  21.4 0.3 shard_map.38
  21.8 95.4 %all-gather.2 = f16[2112,256]{1,0:T(8,128)(2,1)S(1)} all-gather(f16[264,256]{1,0:T(8,128)(2,1)S(1)} %convert_element_type.19), channel_id=2, replica_groups=mesh['parts'=2,'far'=8,'near'=4,'freq'=4,'rep'=2] {'far'}, dimensions={0}, use_global_device_ids=true | all-gather | bytes 1216512 | tf_op jit(solution)/shard_map/all_gather | solution.py:186
  117.2 0.2 convert.turned_ref
  117.4 2.8 %shard_map.39 = (bf16[256,1024]{1,0:T(8,128)(2,1)S(1)}, bf16[128,512]{1,0:T(8,128)(2,1)S(1)}) custom-call(s32[1]{0:T(128)} %bitcast.1.far_ref, f32[8,264,256]{2,1,0:T(8,128)S(1)} %convert.turned_ref, f32[24,2048]{1,0:T(8,128)S(1)} %get-tuple-element.10.cos_ref, f32[24,2048]{1,0:T(8,128)S(1)} %get-tuple-element.9.sin_ref), custom_call_target="tpu_custom_call" | custom-call | tf_op jit(solution)/shard_map/pallas_call | solution.py:158
  120.2 15.9 %all_gather.11.mine_ref = bf16[512,512]{1,0:T(8,128)(2,1)S(1)} all-gather(bf16[128,512]{1,0:T(8,128)(2,1)S(1)} %get-tuple-element.8), channel_id=1, replica_groups=mesh['parts'=2,'far'=8,'near'=4,'freq'=4,'rep'=2] {'near'}, dimensions={0}, use_global_device_ids=true | all-gather | bytes 655360 | tf_op jit(solution)/shard_map/all_gather | solution.py:195
  136.1 1.9 %collective-permute-start = (bf16[512,512]{1,0:T(8,128)(2,1)S(1)}, bf16[512,512]{1,0:T(8,128)(2,1)S(1)}, u32[]{:S(2)}, u32[]{:S(2)}) collective-permute-start(bf16[512,512]{1,0:T(8,128)(2,1)S(1)} %all_gather.11.mine_ref), channel_id=1, source_target_pairs={{0,1},{1,0},{2,3},{3,2},{4,5},{5,4},{6,7},{7,6},{8,9},{9,8},{10,11... | collective-permute-start | bytes 1572872 | tf_op jit(solution)/shard_map/ppermute | solution.py:196
  138.0 1.9 %collective-permute-done.other_ref = bf16[512,512]{1,0:T(8,128)(2,1)S(1)} collective-permute-done((bf16[512,512]{1,0:T(8,128)(2,1)S(1)}, bf16[512,512]{1,0:T(8,128)(2,1)S(1)}, u32[]{:S(2)}, u32[]{:S(2)}) %collective-permute-start) | collective-permute-done | bytes 524320 | tf_op jit(solution)/shard_map/ppermute | solution.py:196
  139.9 0.6 shard_map.40
  140.5 9.2 %all_to_all.10.back_ref = bf16[8,64,128]{2,1,0:T(8,128)(2,1)S(1)} all-to-all(bf16[8,64,128]{2,1,0:T(8,128)(2,1)S(1)} %shard_map.40), channel_id=1, replica_groups=mesh['parts'=2,'far'=8,'near'=4,'freq'=4,'rep'=2] {'near','rep'}, dimensions={0} | all-to-all | bytes 262144 | tf_op jit(solution)/shard_map/all_to_all | solution.py:198
  149.8 2.7 %shard_map.41 = bf16[64,2048]{1,0:T(8,128)(2,1)} custom-call(bf16[8,64,128]{2,1,0:T(8,128)(2,1)S(1)} %all_to_all.10.back_ref, f32[24,2048]{1,0:T(8,128)S(1)} %get-tuple-element.13.cos_ref, f32[24,2048]{1,0:T(8,128)S(1)} %get-tuple-element.14.sin_ref), custom_call_target="tpu_custom_call" | custom-call | tf_op jit(solution)/shard_map/pallas_call | solution.py:158
  (2 shorter events, 0.0 us)
Async XLA Ops:
  2.2 1.0 copy-start
  6.2 15.2 %all-to-all-start = ((bf16[8,64,128]{2,1,0:T(8,128)(2,1)}), bf16[8,64,128]{2,1,0:T(8,128)(2,1)S(1)}, u32[]{:S(2)}, u32[]{:S(2)}) async-start(bf16[8,64,128]{2,1,0:T(8,128)(2,1)} %shard_map.37), calls=%async_computation | async-start | bytes 262144 | tf_op jit(solution)/shard_map/all_to_all | solution.py:184
  136.1 3.8 %collective-permute-start = (bf16[512,512]{1,0:T(8,128)(2,1)S(1)}, bf16[512,512]{1,0:T(8,128)(2,1)S(1)}, u32[]{:S(2)}, u32[]{:S(2)}) collective-permute-start(bf16[512,512]{1,0:T(8,128)(2,1)S(1)} %all_gather.11.mine_ref), channel_id=1, source_target_pairs={{0,1},{1,0},{2,3},{3,2},{4,5},{5,4},{6,7},{7,6},{8,9},{9,8},{10,11... | collective-permute-start | bytes 1572872 | tf_op jit(solution)/shard_map/ppermute | solution.py:196

commit v4 on v3

--- a/solution.py
+++ b/solution.py
@@ -10,7 +10,8 @@
 
 NSLOW = 1024
 FINE = 8
-NEAR = 4
+NEAR = 2
+OWNED = 2
 
 two_pi = 6.283185307179586
 base_hertz = 40.0
@@ -21,7 +22,7 @@
 
 
 def source_row(kind, a, b):
-    return ((b * 2 + kind) * FINE + a) * FINE
+    return (((b // OWNED * 2 + kind) * OWNED + b % OWNED) * FINE + a) * FINE
 
 
 def receiver_row(kind, a, b):
@@ -122,14 +123,7 @@
     inner_ref[half:] = (-both[half:]).astype(jnp.bfloat16)
 
 
-def back_kernel(rep_ref, planes_ref, mine_ref, other_ref, back_ref, inner_ref):
-    rep = rep_ref[0]
-    rows = 2 * FINE * FINE
-    for near in range(NEAR):
-        first = pl.multiple_of((2 * near + rep) * rows, rows)
-        second = pl.multiple_of((2 * near + 1 - rep) * rows, rows)
-        inner_ref[pl.ds(first, rows), :] = mine_ref[near * rows : (near + 1) * rows, :]
-        inner_ref[pl.ds(second, rows), :] = other_ref[near * rows : (near + 1) * rows, :]
+def back_kernel(planes_ref, inner_ref, back_ref):
     total = jnp.dot(planes_ref[...], inner_ref[...], preferred_element_type=jnp.float32)
     upper, lower = split_parts(total, 2.0 / math.sqrt(NSLOW))
     shots = upper.shape[1] // 2
@@ -171,14 +165,14 @@
     near = ("near", "rep")
     peers = lax.axis_size("near") * lax.axis_size("rep")
     around = peers * shots
-    far, rep = [lax.axis_index(name).astype(jnp.int32).reshape(1) for name in ("far", "rep")]
+    far = lax.axis_index("far").astype(jnp.int32).reshape(1)
     omega = two_pi * (base_hertz + step_hertz * lax.axis_index("freq").astype(jnp.float32))
     data = recorded.reshape(2 * shots, receivers)
     receiver_seeds = seeds(omega, receiver_x)
     source_seeds = seeds(omega, source_x)
     receiver_table, source_table = (NSLOW, receivers), (NSLOW, sources)
     columns = 2 * NSLOW // peers
-    chunk = (peers, FINE * FINE, 4 * shots)
+    chunk = (peers, OWNED * FINE * FINE, 4 * shots)
 
     (spread,) = call(forward_kernel, [chunk], [receiver_table], data, *receiver_seeds)
     spread = lax.all_to_all(spread, near, 0, 0, tiled=True)
@@ -192,9 +186,8 @@
         turned,
         *source_seeds,
     )
-    mine = lax.all_gather(inner, "near", axis=0, tiled=True)
-    other = lax.ppermute(mine, "rep", [(0, 1), (1, 0)])
-    (back,) = call(back_kernel, [chunk], [(NSLOW, 2 * around)], rep, planes, mine, other)
+    inner = lax.all_gather(inner, near, axis=0, tiled=True)
+    (back,) = call(back_kernel, [chunk], [], planes, inner)
     back = lax.all_to_all(back, near, 0, 0, tiled=True)
     (out,) = call(inverse_kernel, [(2 * shots, receivers)], [receiver_table], back, *receiver_seeds)
     return out.reshape(recorded.shape)

time: 153 us -> 148 us (0.967)
  the two profiles are of different devices: /device:TPU:42 before, /device:TPU:33 now
where the time goes in v4:
time: 148 us; the launch traced here: 147 us
  blocking collectives  84.5 us (57%)
  starting transfers between devices  44.7 us (30%)
  Pallas kernels  11 us (7%)
  waiting for transfers between devices  3.6 us (2%)
  other arithmetic  2.46 us (2%)
    all_gather x1, blocking collectives, body(): lax.all_gather(turned.astype(jnp.float16), 'far', axis=0, tiled=False)  57.7 us
    all_to_all x1, starting transfers between devices, body(): spread = lax.all_to_all(spread, near, 0, 0, tiled=True)  44.7 us
    all_gather x1, blocking collectives, body(): inner = lax.all_gather(inner, near, axis=0, tiled=True)  20.7 us
    pallas_call x5, Pallas kernels, call(): pl.pallas_call(kernel, out_shape=[jax.ShapeDtypeStruct(shape, dtype) for...  11 us
    all_to_all x1, blocking collectives, body(): back = lax.all_to_all(back, near, 0, 0, tiled=True)  6.16 us
    all_to_all x1, waiting for transfers between devices, body(): spread = lax.all_to_all(spread, near, 0, 0, tiled=True)  3.6 us
  transfers between devices with their start and end apart: 1, of which 1 were waited for; matrix products, arithmetic and copies ran while one was open for 0% of the time, Pallas kernels for 0%

profile of v4, /device:TPU:33, one launch (start us, length us, event | category | flops | bytes accessed | tf_op | source)
XLA Modules:
  0.0 147.3 jit_solution(1206006787888160522)
XLA Ops:
  0.0 2.1 %multiply_sine_fusion = (f32[24,2048]{1,0:T(8,128)S(1)}, f32[24,2048]{1,0:T(8,128)S(1)}, f32[24,2048]{1,0:T(8,128)S(1)}, f32[24,2048]{1,0:T(8,128)S(1)}) fusion(f32[2048]{0:T(1024)} %param.5, f32[24]{0:T(128)S(1)} %fusion.1, f32[2048]{0:T(1024)} %param.4), kind=kLoop, calls=%fused_computation | loop fusion | flops 98304 | bytes 802912 | tf_op jit(solution)/shard_map/sin | solution.py:41
  2.2 0.0 copy-start
  2.2 0.9 copy-done
  3.1 3.0 %shard_map.37 = bf16[4,128,128]{2,1,0:T(8,128)(2,1)} custom-call(bf16[64,2048]{1,0:T(8,128)(2,1)S(1)} %bitcast.7, f32[24,2048]{1,0:T(8,128)S(1)} %get-tuple-element.13.cos_ref, f32[24,2048]{1,0:T(8,128)S(1)} %get-tuple-element.14.sin_ref), custom_call_target="tpu_custom_call" | custom-call | tf_op jit(solution)/shard_map/pallas_call | solution.py:152
  6.2 44.7 %all-to-all-start = ((bf16[4,128,128]{2,1,0:T(8,128)(2,1)}), bf16[4,128,128]{2,1,0:T(8,128)(2,1)S(1)}, u32[]{:S(2)}, u32[]{:S(2)}) async-start(bf16[4,128,128]{2,1,0:T(8,128)(2,1)} %shard_map.37), calls=%async_computation | async-start | bytes 262144 | tf_op jit(solution)/shard_map/all_to_all | solution.py:178
  50.9 3.6 %all-to-all-done.near_ref = bf16[4,128,128]{2,1,0:T(8,128)(2,1)S(1)} async-done(((bf16[4,128,128]{2,1,0:T(8,128)(2,1)}), bf16[4,128,128]{2,1,0:T(8,128)(2,1)S(1)}, u32[]{:S(2)}, u32[]{:S(2)}) %all-to-all-start) | async-done | bytes 131104 | tf_op jit(solution)/shard_map/all_to_all | solution.py:178
  54.5 0.3 shard_map.38
  54.8 57.7 %all-gather.2 = f16[8320,128]{1,0:T(8,128)(2,1)S(1)} all-gather(f16[520,128]{1,0:T(8,128)(2,1)S(1)} %convert_element_type.19), channel_id=2, replica_groups=mesh['parts'=2,'far'=16,'near'=2,'freq'=4,'rep'=2] {'far'}, dimensions={0}, use_global_device_ids=true | all-gather | bytes 2263040 | tf_op jit(solution)/shard_map/all_gather | solution.py:180
  112.5 0.3 convert.turned_ref
  112.8 4.4 %shard_map.39 = (bf16[512,1024]{1,0:T(8,128)(2,1)S(1)}, bf16[256,256]{1,0:T(8,128)(2,1)S(1)}) custom-call(s32[1]{0:T(128)} %bitcast.far_ref, f32[16,520,128]{2,1,0:T(8,128)S(1)} %convert.turned_ref, f32[24,2048]{1,0:T(8,128)S(1)} %get-tuple-element.10.cos_ref, f32[24,2048]{1,0:T(8,128)S(1)} %get-tuple-element.9.sin_ref), custom_call_target="tpu_custom_call" | custom-call | tf_op jit(solution)/shard_map/pallas_call | solution.py:152
  117.3 20.7 %all_gather.11.inner_ref = bf16[1024,256]{1,0:T(8,128)(2,1)S(1)} all-gather(bf16[256,256]{1,0:T(8,128)(2,1)S(1)} %get-tuple-element.8), channel_id=1, replica_groups=mesh['parts'=2,'far'=16,'near'=2,'freq'=4,'rep'=2] {'near','rep'}, dimensions={0}, use_global_device_ids=true | all-gather | bytes 655360 | tf_op jit(solution)/shard_map/all_gather | solution.py:189
  137.9 0.5 shard_map.40
  138.5 6.2 %all_to_all.10.back_ref = bf16[4,128,128]{2,1,0:T(8,128)(2,1)S(1)} all-to-all(bf16[4,128,128]{2,1,0:T(8,128)(2,1)S(1)} %shard_map.40), channel_id=1, replica_groups=mesh['parts'=2,'far'=16,'near'=2,'freq'=4,'rep'=2] {'near','rep'}, dimensions={0} | all-to-all | bytes 262144 | tf_op jit(solution)/shard_map/all_to_all | solution.py:191
  144.6 2.7 %shard_map.41 = bf16[64,2048]{1,0:T(8,128)(2,1)} custom-call(bf16[4,128,128]{2,1,0:T(8,128)(2,1)S(1)} %all_to_all.10.back_ref, f32[24,2048]{1,0:T(8,128)S(1)} %get-tuple-element.13.cos_ref, f32[24,2048]{1,0:T(8,128)S(1)} %get-tuple-element.14.sin_ref), custom_call_target="tpu_custom_call" | custom-call | tf_op jit(solution)/shard_map/pallas_call | solution.py:152
  (2 shorter events, 0.0 us)
Async XLA Ops:
  2.2 1.0 copy-start
  6.2 48.3 %all-to-all-start = ((bf16[4,128,128]{2,1,0:T(8,128)(2,1)}), bf16[4,128,128]{2,1,0:T(8,128)(2,1)S(1)}, u32[]{:S(2)}, u32[]{:S(2)}) async-start(bf16[4,128,128]{2,1,0:T(8,128)(2,1)} %shard_map.37), calls=%async_computation | async-start | bytes 262144 | tf_op jit(solution)/shard_map/all_to_all | solution.py:178

commit v5 on v4

--- a/solution.py
+++ b/solution.py
@@ -41,32 +41,39 @@
     return jnp.cos(phases), jnp.sin(phases)
 
 
-def fill_table(cos_ref, sin_ref, table_ref, row_of):
-    width = min(256, table_ref.shape[1])
-
-    def fill(step, carry):
-        lanes = pl.ds(pl.multiple_of(step * width, width), width)
-        c0, s0 = cos_ref[0:FINE, lanes], sin_ref[0:FINE, lanes]
-        inner = [(c0, s0)]
-        for b in range(1, FINE):
-            cb, sb = cos_ref[pl.ds(FINE + b, 1), lanes], sin_ref[pl.ds(FINE + b, 1), lanes]
-            inner.append((c0 * cb - s0 * sb, s0 * cb + c0 * sb))
-        for a in range(0, FINE, 2):
-            turns = [
-                (cos_ref[pl.ds(2 * FINE + k, 1), lanes], sin_ref[pl.ds(2 * FINE + k, 1), lanes]) for k in (a, a + 1)
-            ]
-            for b, (c, s) in enumerate(inner):
-                pairs = [(c * ca - s * sa, s * ca + c * sa) for ca, sa in turns]
-                for kind in range(2):
-                    rows = jnp.concatenate([pair[kind] for pair in pairs], axis=0).astype(jnp.bfloat16)
-                    table_ref[pl.ds(row_of(kind, a, b), 2 * FINE), lanes] = rows
-        return carry
-
-    lax.fori_loop(0, table_ref.shape[1] // width, fill, 0)
+WIDTH = 256
+
+
+def fill_lanes(cos_ref, sin_ref, table_ref, row_of, first):
+    lanes = pl.ds(first, WIDTH)
+    c0, s0 = cos_ref[0:FINE, lanes], sin_ref[0:FINE, lanes]
+    inner = [(c0, s0)]
+    for b in range(1, FINE):
+        cb, sb = cos_ref[pl.ds(FINE + b, 1), lanes], sin_ref[pl.ds(FINE + b, 1), lanes]
+        inner.append((c0 * cb - s0 * sb, s0 * cb + c0 * sb))
+    for a in range(0, FINE, 2):
+        turns = [(cos_ref[pl.ds(2 * FINE + k, 1), lanes], sin_ref[pl.ds(2 * FINE + k, 1), lanes]) for k in (a, a + 1)]
+        for b, (c, s) in enumerate(inner):
+            pairs = [(c * ca - s * sa, s * ca + c * sa) for ca, sa in turns]
+            for kind in range(2):
+                rows = jnp.concatenate([pair[kind] for pair in pairs], axis=0).astype(jnp.bfloat16)
+                table_ref[pl.ds(row_of(kind, a, b), 2 * FINE), lanes] = rows
 
 
 def dot_last(left, right):
     return lax.dot_general(left, right, (((1,), (1,)), ((), ())), preferred_element_type=jnp.float32)
+
+
+def filled_product(cos_ref, sin_ref, table_ref, row_of, right_ref, pieces):
+    span = table_ref.shape[1] // pieces
+    total = None
+    for start in range(0, table_ref.shape[1], span):
+        for first in range(start, start + span, WIDTH):
+            fill_lanes(cos_ref, sin_ref, table_ref, row_of, first)
+        lanes = slice(start, start + span)
+        piece = dot_last(table_ref[:, lanes], right_ref[:, lanes])
+        total = piece if total is None else total + piece
+    return total * (1.0 / math.sqrt(table_ref.shape[1]))
 
 
 def split_parts(x, scale):
@@ -76,8 +83,7 @@
 
 
 def forward_kernel(data_ref, cos_ref, sin_ref, spread_ref, table_ref):
-    fill_table(cos_ref, sin_ref, table_ref, receiver_row)
-    total = dot_last(table_ref[...], data_ref[...]) * (1.0 / math.sqrt(data_ref.shape[1]))
+    total = filled_product(cos_ref, sin_ref, table_ref, receiver_row, data_ref, 4)
     half = total.shape[0] // 2
     both = jnp.concatenate([total[:half], total[half:]], axis=1)
     spread_ref[...] = both.reshape(spread_ref.shape).astype(jnp.bfloat16)
@@ -105,14 +111,13 @@
 
 
 def planes_kernel(far_ref, turned_ref, cos_ref, sin_ref, planes_ref, inner_ref, table_ref, spread_ref):
-    fill_table(cos_ref, sin_ref, table_ref, source_row)
     peers, _, around = turned_ref.shape
     main = spread_ref.shape[0]
     for far in range(peers):
         block = turned_ref[far].astype(jnp.float32)
         block = block[:main] * jnp.exp2(block[main : main + 1, :1] - LEVEL)
         spread_ref[:, far * around : (far + 1) * around] = block.astype(jnp.bfloat16)
-    total = dot_last(table_ref[...], spread_ref[...]) * (1.0 / math.sqrt(table_ref.shape[1]))
+    total = filled_product(cos_ref, sin_ref, table_ref, source_row, spread_ref, 2)
     planes = total.T.astype(jnp.bfloat16)
     planes_ref[...] = planes
     own = table_ref[:, pl.ds(pl.multiple_of(far_ref[0] * around, around), around)]
@@ -138,12 +143,14 @@
 
 
 def inverse_kernel(back_ref, cos_ref, sin_ref, out_ref, table_ref):
-    fill_table(cos_ref, sin_ref, table_ref, receiver_row)
     peers, half, lanes = back_ref.shape
     turned = back_ref[...].astype(jnp.float32).reshape(peers * half, lanes).T
     back = jnp.concatenate([turned[: lanes // 2], turned[lanes // 2 :]], axis=1).astype(jnp.bfloat16)
-    total = jnp.dot(back, table_ref[...], preferred_element_type=jnp.float32)
-    out_ref[...] = (total * (2.0 / math.sqrt(NSLOW))).astype(jnp.bfloat16)
+    for first in range(0, table_ref.shape[1], WIDTH):
+        fill_lanes(cos_ref, sin_ref, table_ref, receiver_row, first)
+        lanes = slice(first, first + WIDTH)
+        total = jnp.dot(back, table_ref[:, lanes], preferred_element_type=jnp.float32)
+        out_ref[:, lanes] = (total * (2.0 / math.sqrt(NSLOW))).astype(jnp.bfloat16)
 
 
 def call(kernel, shapes, scratch, *operands, dtype=jnp.bfloat16):
@@ -169,13 +176,14 @@
     omega = two_pi * (base_hertz + step_hertz * lax.axis_index("freq").astype(jnp.float32))
     data = recorded.reshape(2 * shots, receivers)
     receiver_seeds = seeds(omega, receiver_x)
-    source_seeds = seeds(omega, source_x)
     receiver_table, source_table = (NSLOW, receivers), (NSLOW, sources)
     columns = 2 * NSLOW // peers
     chunk = (peers, OWNED * FINE * FINE, 4 * shots)
 
     (spread,) = call(forward_kernel, [chunk], [receiver_table], data, *receiver_seeds)
+    spread, source_x = lax.optimization_barrier((spread, source_x))
     spread = lax.all_to_all(spread, near, 0, 0, tiled=True)
+    source_seeds = seeds(omega, source_x)
     (turned,) = call(turn_kernel, [(columns + FINE, around)], [], spread, dtype=jnp.float32)
     turned = lax.all_gather(turned.astype(jnp.float16), "far", axis=0, tiled=False).astype(jnp.float32)
     planes, inner = call(

time: 148 us -> 146 us (0.986)
  Pallas kernels: 11 us -> 8.54 us
  blocking collectives: 84.5 us -> 86.2 us
    pallas_call x5, Pallas kernels: 11 us -> 8.54 us  [call(): pl.pallas_call(kernel, out_shape=[jax.ShapeDtypeStruct(shape, dtype) for...]
    all_gather x1, blocking collectives: 57.7 us -> 59.5 us  [body(): lax.all_gather(turned.astype(jnp.float16), 'far', axis=0, tiled=False)]
  transfers between devices with their start and end apart: 1 -> 1, of which waited for: 1 -> 1; matrix products, arithmetic and copies ran while one was open for 0% -> 1% of each run, Pallas kernels for 0% -> 0%
where the time goes in v5:
time: 146 us
  blocking collectives  86.2 us (59%)
  starting transfers between devices  44.7 us (31%)
  Pallas kernels  8.54 us (6%)
  other arithmetic  3.22 us (2%)
  waiting for transfers between devices  2.14 us (1%)
    all_gather x1, blocking collectives, body(): lax.all_gather(turned.astype(jnp.float16), 'far', axis=0, tiled=False)  59.5 us
    all_to_all x1, starting transfers between devices, body(): spread = lax.all_to_all(spread, near, 0, 0, tiled=True)  44.7 us
    all_gather x1, blocking collectives, body(): inner = lax.all_gather(inner, near, axis=0, tiled=True)  20.5 us
    pallas_call x5, Pallas kernels, call(): pl.pallas_call(kernel, out_shape=[jax.ShapeDtypeStruct(shape, dtype) for...  8.54 us
    all_to_all x1, blocking collectives, body(): back = lax.all_to_all(back, near, 0, 0, tiled=True)  6.16 us
  transfers between devices with their start and end apart: 1, of which 1 were waited for; matrix products, arithmetic and copies ran while one was open for 1% of the time, Pallas kernels for 0%

profile of v5, /device:TPU:33, one launch (start us, length us, event | category | flops | bytes accessed | tf_op | source)
XLA Modules:
  0.0 145.8 jit_solution(141667623591463955)
XLA Ops:
  0.0 1.5 %multiply_sine_fusion.1 = (f32[24,2048]{1,0:T(8,128)S(1)}, f32[24,2048]{1,0:T(8,128)S(1)}) fusion(f32[2048]{0:T(1024)} %param.4, f32[24]{0:T(128)S(1)} %fusion.1), kind=kLoop, calls=%fused_computation.2 | loop fusion | flops 49152 | bytes 401504 | tf_op jit(solution)/shard_map/sin | solution.py:41
  1.5 0.0 copy-start
  1.5 0.9 copy-done
  2.4 2.0 %shard_map.37 = bf16[4,128,128]{2,1,0:T(8,128)(2,1)} custom-call(bf16[64,2048]{1,0:T(8,128)(2,1)S(1)} %bitcast.7, f32[24,2048]{1,0:T(8,128)S(1)} %get-tuple-element.16.cos_ref, f32[24,2048]{1,0:T(8,128)S(1)} %get-tuple-element.15.sin_ref), custom_call_target="tpu_custom_call" | custom-call | tf_op jit(solution)/shard_map/pallas_call | solution.py:159
  4.5 44.7 %all-to-all-start = ((bf16[4,128,128]{2,1,0:T(8,128)(2,1)}), bf16[4,128,128]{2,1,0:T(8,128)(2,1)S(1)}, u32[]{:S(2)}, u32[]{:S(2)}) async-start(bf16[4,128,128]{2,1,0:T(8,128)(2,1)} %shard_map.37), calls=%async_computation | async-start | bytes 262144 | tf_op jit(solution)/shard_map/all_to_all | solution.py:185
  49.2 1.5 multiply_sine_fusion
  50.6 2.1 %all-to-all-done.near_ref = bf16[4,128,128]{2,1,0:T(8,128)(2,1)S(1)} async-done(((bf16[4,128,128]{2,1,0:T(8,128)(2,1)}), bf16[4,128,128]{2,1,0:T(8,128)(2,1)S(1)}, u32[]{:S(2)}, u32[]{:S(2)}) %all-to-all-start) | async-done | bytes 131104 | tf_op jit(solution)/shard_map/all_to_all | solution.py:185
  52.8 0.3 shard_map.38
  53.1 59.5 %all-gather.2 = f16[8320,128]{1,0:T(8,128)(2,1)S(1)} all-gather(f16[520,128]{1,0:T(8,128)(2,1)S(1)} %convert_element_type.19), channel_id=2, replica_groups=mesh['parts'=2,'far'=16,'near'=2,'freq'=4,'rep'=2] {'far'}, dimensions={0}, use_global_device_ids=true | all-gather | bytes 2263040 | tf_op jit(solution)/shard_map/all_gather | solution.py:188
  112.6 0.3 convert.turned_ref
  112.9 3.5 %shard_map.39 = (bf16[512,1024]{1,0:T(8,128)(2,1)S(1)}, bf16[256,256]{1,0:T(8,128)(2,1)S(1)}) custom-call(s32[1]{0:T(128)} %bitcast.far_ref, f32[16,520,128]{2,1,0:T(8,128)S(1)} %convert.turned_ref, f32[24,2048]{1,0:T(8,128)S(1)} %get-tuple-element.14.cos_ref, f32[24,2048]{1,0:T(8,128)S(1)} %get-tuple-element.13.sin_ref), custom_call_target="tpu_custom_call" | custom-call | tf_op jit(solution)/shard_map/pallas_call | solution.py:159
  116.4 20.5 %all_gather.11.inner_ref = bf16[1024,256]{1,0:T(8,128)(2,1)S(1)} all-gather(bf16[256,256]{1,0:T(8,128)(2,1)S(1)} %get-tuple-element.12), channel_id=1, replica_groups=mesh['parts'=2,'far'=16,'near'=2,'freq'=4,'rep'=2] {'near','rep'}, dimensions={0}, use_global_device_ids=true | all-gather | bytes 655360 | tf_op jit(solution)/shard_map/all_gather | solution.py:197
  137.0 0.5 shard_map.40
  137.5 6.2 %all_to_all.10.back_ref = bf16[4,128,128]{2,1,0:T(8,128)(2,1)S(1)} all-to-all(bf16[4,128,128]{2,1,0:T(8,128)(2,1)S(1)} %shard_map.40), channel_id=1, replica_groups=mesh['parts'=2,'far'=16,'near'=2,'freq'=4,'rep'=2] {'near','rep'}, dimensions={0} | all-to-all | bytes 262144 | tf_op jit(solution)/shard_map/all_to_all | solution.py:199
  143.7 2.1 %shard_map.41 = bf16[64,2048]{1,0:T(8,128)(2,1)} custom-call(bf16[4,128,128]{2,1,0:T(8,128)(2,1)S(1)} %all_to_all.10.back_ref, f32[24,2048]{1,0:T(8,128)S(1)} %get-tuple-element.16.cos_ref, f32[24,2048]{1,0:T(8,128)S(1)} %get-tuple-element.15.sin_ref), custom_call_target="tpu_custom_call" | custom-call | tf_op jit(solution)/shard_map/pallas_call | solution.py:159
  (2 shorter events, 0.0 us)
Async XLA Ops:
  1.5 1.0 copy-start
  4.5 48.3 %all-to-all-start = ((bf16[4,128,128]{2,1,0:T(8,128)(2,1)}), bf16[4,128,128]{2,1,0:T(8,128)(2,1)S(1)}, u32[]{:S(2)}, u32[]{:S(2)}) async-start(bf16[4,128,128]{2,1,0:T(8,128)(2,1)} %shard_map.37), calls=%async_computation | async-start | bytes 262144 | tf_op jit(solution)/shard_map/all_to_all | solution.py:185

commit v6 on v5

--- a/solution.py
+++ b/solution.py
@@ -185,7 +185,9 @@
     spread = lax.all_to_all(spread, near, 0, 0, tiled=True)
     source_seeds = seeds(omega, source_x)
     (turned,) = call(turn_kernel, [(columns + FINE, around)], [], spread, dtype=jnp.float32)
-    turned = lax.all_gather(turned.astype(jnp.float16), "far", axis=0, tiled=False).astype(jnp.float32)
+    block = turned.shape
+    turned = lax.all_gather(turned.astype(jnp.float16).reshape(-1), "far", axis=0, tiled=True)
+    turned = turned.reshape(-1, *block).astype(jnp.float32)
     planes, inner = call(
         planes_kernel,
         [(columns, NSLOW), (columns // 2, 2 * around)],

time: 146 us -> 146 us (level)
  no operation moved by 1% of the time
where the time goes in v6:
time: 146 us
  blocking collectives  86.2 us (59%)
  starting transfers between devices  44.7 us (31%)
  Pallas kernels  8.54 us (6%)
  other arithmetic  3.22 us (2%)
  waiting for transfers between devices  2.14 us (1%)
    all_gather x1, blocking collectives, body(): lax.all_gather(turned.astype(jnp.float16).reshape(-1), 'far', axis=0, til...  59.5 us
    all_to_all x1, starting transfers between devices, body(): spread = lax.all_to_all(spread, near, 0, 0, tiled=True)  44.7 us
    all_gather x1, blocking collectives, body(): inner = lax.all_gather(inner, near, axis=0, tiled=True)  20.5 us
    pallas_call x5, Pallas kernels, call(): pl.pallas_call(kernel, out_shape=[jax.ShapeDtypeStruct(shape, dtype) for...  8.54 us
    all_to_all x1, blocking collectives, body(): back = lax.all_to_all(back, near, 0, 0, tiled=True)  6.16 us
  transfers between devices with their start and end apart: 1, of which 1 were waited for; matrix products, arithmetic and copies ran while one was open for 1% of the time, Pallas kernels for 0%

profile of v6, /device:TPU:33, one launch (start us, length us, event | category | flops | bytes accessed | tf_op | source)
XLA Modules:
  0.0 145.8 jit_solution(16637482922379787559)
XLA Ops:
  0.0 1.5 %multiply_sine_fusion.1 = (f32[24,2048]{1,0:T(8,128)S(1)}, f32[24,2048]{1,0:T(8,128)S(1)}) fusion(f32[2048]{0:T(1024)} %param.4, f32[24]{0:T(128)S(1)} %fusion.1), kind=kLoop, calls=%fused_computation.2 | loop fusion | flops 49152 | bytes 401504 | tf_op jit(solution)/shard_map/sin | solution.py:41
  1.5 0.0 copy-start
  1.5 0.9 copy-done
  2.4 2.0 %shard_map.37 = bf16[4,128,128]{2,1,0:T(8,128)(2,1)} custom-call(bf16[64,2048]{1,0:T(8,128)(2,1)S(1)} %bitcast.9, f32[24,2048]{1,0:T(8,128)S(1)} %get-tuple-element.16.cos_ref, f32[24,2048]{1,0:T(8,128)S(1)} %get-tuple-element.15.sin_ref), custom_call_target="tpu_custom_call" | custom-call | tf_op jit(solution)/shard_map/pallas_call | solution.py:159
  4.5 44.7 %all-to-all-start = ((bf16[4,128,128]{2,1,0:T(8,128)(2,1)}), bf16[4,128,128]{2,1,0:T(8,128)(2,1)S(1)}, u32[]{:S(2)}, u32[]{:S(2)}) async-start(bf16[4,128,128]{2,1,0:T(8,128)(2,1)} %shard_map.37), calls=%async_computation | async-start | bytes 262144 | tf_op jit(solution)/shard_map/all_to_all | solution.py:185
  49.2 1.5 multiply_sine_fusion
  50.6 2.1 %all-to-all-done.near_ref = bf16[4,128,128]{2,1,0:T(8,128)(2,1)S(1)} async-done(((bf16[4,128,128]{2,1,0:T(8,128)(2,1)}), bf16[4,128,128]{2,1,0:T(8,128)(2,1)S(1)}, u32[]{:S(2)}, u32[]{:S(2)}) %all-to-all-start) | async-done | bytes 131104 | tf_op jit(solution)/shard_map/all_to_all | solution.py:185
  52.8 0.3 shard_map.38
  53.1 59.5 %all-gather.1 = f16[1064960]{0:T(1024)(128)(2,1)S(1)} all-gather(f16[66560]{0:T(1024)(128)(2,1)S(1)} %convert_bitcast_fusion), channel_id=1, replica_groups=mesh['parts'=2,'far'=16,'near'=2,'freq'=4,'rep'=2] {'far'}, dimensions={0}, use_global_device_ids=true | all-gather | bytes 2263040 | tf_op jit(solution)/shard_map/all_gather | solution.py:189
  112.6 0.3 convert.1.turned_ref
  112.9 3.5 %shard_map.39 = (bf16[512,1024]{1,0:T(8,128)(2,1)S(1)}, bf16[256,256]{1,0:T(8,128)(2,1)S(1)}) custom-call(s32[1]{0:T(128)} %bitcast.far_ref, f32[16,520,128]{2,1,0:T(8,128)S(1)} %convert.1.turned_ref, f32[24,2048]{1,0:T(8,128)S(1)} %get-tuple-element.14.cos_ref, f32[24,2048]{1,0:T(8,128)S(1)} %get-tuple-element.13.sin_ref), custom_call_target="tpu_custom_call" | custom-call | tf_op jit(solution)/shard_map/pallas_call | solution.py:159
  116.4 20.5 %all_gather.7.inner_ref = bf16[1024,256]{1,0:T(8,128)(2,1)S(1)} all-gather(bf16[256,256]{1,0:T(8,128)(2,1)S(1)} %get-tuple-element.12), channel_id=1, replica_groups=mesh['parts'=2,'far'=16,'near'=2,'freq'=4,'rep'=2] {'near','rep'}, dimensions={0}, use_global_device_ids=true | all-gather | bytes 655360 | tf_op jit(solution)/shard_map/all_gather | solution.py:199
  137.0 0.5 shard_map.40
  137.5 6.2 %all_to_all.10.back_ref = bf16[4,128,128]{2,1,0:T(8,128)(2,1)S(1)} all-to-all(bf16[4,128,128]{2,1,0:T(8,128)(2,1)S(1)} %shard_map.40), channel_id=1, replica_groups=mesh['parts'=2,'far'=16,'near'=2,'freq'=4,'rep'=2] {'near','rep'}, dimensions={0} | all-to-all | bytes 262144 | tf_op jit(solution)/shard_map/all_to_all | solution.py:201
  143.6 2.1 %shard_map.41 = bf16[64,2048]{1,0:T(8,128)(2,1)} custom-call(bf16[4,128,128]{2,1,0:T(8,128)(2,1)S(1)} %all_to_all.10.back_ref, f32[24,2048]{1,0:T(8,128)S(1)} %get-tuple-element.16.cos_ref, f32[24,2048]{1,0:T(8,128)S(1)} %get-tuple-element.15.sin_ref), custom_call_target="tpu_custom_call" | custom-call | tf_op jit(solution)/shard_map/pallas_call | solution.py:159
  (2 shorter events, 0.0 us)
Async XLA Ops:
  1.5 1.0 copy-start
  4.5 48.3 %all-to-all-start = ((bf16[4,128,128]{2,1,0:T(8,128)(2,1)}), bf16[4,128,128]{2,1,0:T(8,128)(2,1)S(1)}, u32[]{:S(2)}, u32[]{:S(2)}) async-start(bf16[4,128,128]{2,1,0:T(8,128)(2,1)} %shard_map.37), calls=%async_computation | async-start | bytes 262144 | tf_op jit(solution)/shard_map/all_to_all | solution.py:185
